TPU v7x, 256 devices: a whole 4x4x8 slice. The times are simulated.
256 devices in a mesh: member: 64 (over y, z, core), region: 4 (over x).
Axes of the slice: x: 4, y: 4, z: 8, core: 2. Of those that a mesh axis runs over, the one named last changes fastest.
Arguments:
- ensemble: bfloat16 [512, 262144], P(('member', 'region')), may hold values from -12 to 12
- obs_offset: int32 [4, 64, 16], P('region', 'member'), may hold values from 0 to 1023
- observed: float32 [4, 64, 16], P('region', 'member'), may hold values from -12 to 12
- obs_var: float32 [4, 64, 16], P('region', 'member'), may hold values from 0.2 to 2
Outputs:
- analysis: bfloat16 [512, 262144], P(('member', 'region'))
Inputs may be any that keep to these rules, and one draw needn't show every extreme that they name: obs_offset indexes a link within the block of 1024 links; two detectors may watch the same link.
All inputs are finite; a program needn't handle non-finite values.
Results may differ from a plain program's by a relative error of at most 0.0019.
Values may be sent and summed in bfloat16 or wider, within the bound.
A program may use at most 128 MiB of HBM per device.

v0:
```python
import jax
import jax.numpy as jnp
from jax import lax
from jax.experimental import pallas as pl
from jax.experimental.pallas import tpu as pltpu
from jax.sharding import Mesh
from jax.sharding import PartitionSpec as P

MEMBER = ("member_0", "member_1", "member_2")
REGION_MEMBER = ("region", "member_0", "member_1", "member_2")
MEMBER_REGION = ("member_0", "member_1", "member_2", "region")


def split_up(x, dim, devices):
    dims = x.shape
    pieces = x.reshape(*dims[:dim], devices, dims[dim] // devices, *dims[dim + 1 :])
    return jnp.moveaxis(pieces, dim, 0)


def laid_out(pieces, dim):
    pieces = jnp.moveaxis(pieces, 0, dim)
    dims = pieces.shape
    return pieces.reshape(*dims[:dim], dims[dim] * dims[dim + 1], *dims[dim + 2 :])


def one_exchange(x, axis, axes, splits, concats):
    sizes = [lax.axis_size(a) for a in axes]
    pieces = split_up(x, splits[0], sizes[0])
    pieces = jnp.moveaxis(split_up(pieces, splits[1] + 1, sizes[1]), 0, 1)
    inside = pieces.shape[2:]
    pieces = pieces.reshape(-1, *inside)
    pieces = lax.all_to_all(pieces, axis, split_axis=0, concat_axis=0, tiled=True)
    pieces = laid_out(pieces.reshape(*sizes, *inside), concats[0] + 1)
    return laid_out(pieces, concats[1])


def sent_and_summed(x, axis, dim):
    devices = lax.axis_size(axis)
    pieces = lax.all_to_all(split_up(x, dim, devices), axis, 0, 0, tiled=True)
    return jnp.sum(pieces, axis=0)


def sum_by_axis(x, axes, dim):
    far, near = axes
    pieces = split_up(x, dim, lax.axis_size(far))
    nearer = sent_and_summed(pieces, near, dim + 1)
    arrived = lax.all_to_all(nearer, far, split_axis=0, concat_axis=0, tiled=True)
    return arrived.sum(axis=0)


def rows_for(lines, devices):
    spare = -len(lines) % devices
    return jnp.pad(lines, [(0, spare)] + [(0, 0)] * (lines.ndim - 1))


def from_everyone(x, axis):
    devices = lax.axis_size(axis)
    return lax.all_to_all(jnp.broadcast_to(x[None], (devices, *x.shape)), axis, 0, 0, tiled=True)


def whole_of(x, axes, dim):
    far, near = axes
    first = from_everyone(x, far)
    pieces = jnp.swapaxes(from_everyone(first, near), 0, 1)
    return laid_out(pieces.reshape(-1, *x.shape), dim)


def sum_by_parts(x, axes):
    own = sum_by_axis(rows_for(x, lax.axis_size(axes[0]) * lax.axis_size(axes[1])), axes, 0)
    whole = whole_of(own, axes, 0)
    return whole[: len(x)].reshape(x.shape)


def together(arrays, axis):
    ends = [0]
    for a in arrays:
        ends.append(ends[-1] + a.size)
    total = sum_by_parts(jnp.concatenate([a.ravel() for a in arrays]), axis)
    return tuple((total[b:e].reshape(a.shape) for a, b, e in zip(arrays, ends, ends[1:])))


def observation_terms(picked, values, variance, ensemble_size):
    center = jnp.mean(picked, axis=1, keepdims=True)
    anomaly = picked - center
    innovation = values - center[:, 0]
    numer = jnp.sum(innovation * innovation)
    denom = jnp.sum(jnp.sum(anomaly * anomaly, axis=1) / (ensemble_size - 1.0) + variance)
    weight = 1.0 / ((ensemble_size - 1.0) * variance)
    return (anomaly, innovation, weight, numer, denom)


def weighted_products(anomaly, innovation, weight):
    weighted = anomaly * weight[:, None]
    products = jnp.dot(weighted.T, anomaly, precision=lax.Precision.HIGHEST)
    column = jnp.dot(innovation * weight, anomaly, precision=lax.Precision.HIGHEST)
    return (products, column)


def split_bf16(a):
    high = a.astype(jnp.bfloat16)
    return high, (a - high.astype(jnp.float32)).astype(jnp.bfloat16)


def dot1(a, b):
    return jnp.dot(
        a.astype(jnp.bfloat16), b.astype(jnp.bfloat16), preferred_element_type=jnp.float32
    )


def dot3(a, b):
    ah, al = split_bf16(a)
    bh, bl = split_bf16(b)
    return dot1(ah, bh) + (dot1(ah, bl) + dot1(al, bh))


def dot6(a, b):
    return jnp.dot(a, b, precision=lax.Precision.HIGHEST, preferred_element_type=jnp.float32)


TILE = 128
WELL_CONDITIONED = 600.0
ROUNDING = 1e-6


def by_rows(rows, body, init=None):
    def step(i, carry):
        return body(pl.ds(pl.multiple_of(i * TILE, TILE), TILE), carry)

    return lax.fori_loop(0, rows // TILE, step, init)


def largest_row(m):
    return jnp.max(jnp.sum(jnp.abs(m), axis=1))


def sum_of_squares(m):
    return jnp.sum(m * m)


def unit(rows, n):
    row = lax.broadcasted_iota(jnp.int32, (TILE, n), 0) + rows.start
    col = lax.broadcasted_iota(jnp.int32, (TILE, n), 1)
    return jnp.where(row == col, 1.0, 0.0).astype(jnp.float32)


def inverse_into(x, system, r, tmp):
    n = system.shape[0]

    def series(dot, enough):
        def square(rows, bound):
            tmp[rows, :] = dot(system[rows, :], system[...])
            return jnp.maximum(bound, largest_row(tmp[rows, :]))

        bound = jnp.sqrt(by_rows(n, square, jnp.float32(0.0)) * 1.02)
        a = 2.0 / (1.0 + bound)

        def first(rows, total):
            eye = unit(rows, n)
            s = system[rows, :] * a
            x[rows, :] = a * (2.0 * eye - s)
            left = eye - 2.0 * s + (a * a) * tmp[rows, :]
            r[rows, :] = left
            return total + sum_of_squares(left)

        size = by_rows(n, first, jnp.float32(0.0))

        def more(state):
            count, size = state
            return jnp.logical_and(count < 40, size > enough * enough)

        def double(state):
            count, _ = state

            def grow(rows, _):
                x[rows, :] += dot(x[rows, :], r[...])
                tmp[rows, :] = dot(r[rows, :], r[...])
                return 0

            by_rows(n, grow, 0)

            def take(rows, total):
                left = tmp[rows, :]
                r[rows, :] = left
                return total + sum_of_squares(left)

            return count + 1, by_rows(n, take, jnp.float32(0.0))

        lax.while_loop(more, double, (jnp.int32(0), size))

    def newton(dot, dot_step):
        def more(state):
            count, size = state
            return jnp.logical_and(count < 12, size > ROUNDING)

        def step(state):
            count, _ = state

            def residual(rows, total):
                left = unit(rows, n) - dot(system[rows, :], x[...])
                r[rows, :] = left
                return total + sum_of_squares(left)

            size = by_rows(n, residual, jnp.float32(0.0))

            def correct(rows, _):
                x[rows, :] += dot_step(x[rows, :], r[...])
                return 0

            by_rows(n, correct, 0)
            return count + 1, size

        return lax.while_loop(more, step, (jnp.int32(0), jnp.float32(1.0)))[1]

    bound = by_rows(n, lambda rows, m: jnp.maximum(m, largest_row(system[rows, :])), jnp.float32(0.0))
    easy = bound < WELL_CONDITIONED

    def quick():
        series(dot1, 0.1)
        return newton(dot3, dot3)

    left = lax.cond(easy, quick, lambda: jnp.float32(1.0))

    @pl.when(jnp.logical_not(left <= ROUNDING))
    def _():
        series(dot6, 0.02)
        newton(dot6, dot6)


def analysis_kernel(products, column, sums, state, out, x, system, r, tmp):
    n = products.shape[0]
    square = sums[0] / sums[1]
    inflation = jnp.sqrt(jnp.full((1, n), square, jnp.float32))

    def scaled(rows, trace):
        eye = unit(rows, n)
        p = products[rows, :] * square
        system[rows, :] = eye + p
        return trace + jnp.sum(eye * p)

    trace = by_rows(n, scaled, jnp.float32(0.0))
    shift = trace / ((n - 1.0) * n)

    def shifted(rows, _):
        system[rows, :] += shift
        return 0

    by_rows(n, shifted, 0)
    inverse_into(x, system, r, tmp)

    q = dot6(column[...], x[...])

    def mix(rows, _):
        eye = unit(rows, n)
        mixing = 0.5 * inflation * (eye + x[rows, :]) + square * q
        mean = jnp.sum(mixing, axis=1, keepdims=True) * (1.0 / n)
        high, low = split_bf16(mixing - mean + 1.0 / n)
        out[rows, :] = (dot1(high, state[...]) + dot1(low, state[...])).astype(jnp.bfloat16)
        return 0

    by_rows(n, mix, 0)


def analysed(products, column, numer, denom, state):
    n = products.shape[0]
    sums = jnp.stack([numer, denom])
    vmem = pl.BlockSpec(memory_space=pltpu.VMEM)
    return pl.pallas_call(
        analysis_kernel,
        name="analysis",
        out_shape=jax.ShapeDtypeStruct(state.shape, jnp.bfloat16),
        in_specs=[vmem, vmem, pl.BlockSpec(memory_space=pltpu.SMEM), vmem],
        out_specs=vmem,
        scratch_shapes=[pltpu.VMEM((n, n), jnp.float32) for _ in range(4)],
    )(products, column[None, :], sums, state)


def local(ensemble, obs_offset, observed, obs_var):
    members = lax.axis_size(MEMBER)
    regions = lax.axis_size("region")
    own_count = ensemble.shape[0]
    ensemble_size = own_count * members * regions
    shifted = one_exchange(ensemble, REGION_MEMBER, ("region", MEMBER), (1, 1), (0, 0))
    offsets = obs_offset.reshape(-1)
    values = observed.reshape(-1)
    variance = obs_var.reshape(-1)
    picked = jnp.take(shifted, offsets, axis=1).T.astype(jnp.float32)
    anomaly, innovation, weight, numer, denom = observation_terms(
        picked, values, variance, ensemble_size
    )
    products, column = weighted_products(anomaly, innovation, weight)
    products, column, numer, denom = together(
        (products, column, numer, denom), (("member_0", "member_1"), ("member_2", "region"))
    )
    updated = analysed(products, column, numer, denom, shifted)
    return one_exchange(updated, MEMBER_REGION, (MEMBER, "region"), (0, 0), (1, 1))


def solution(mesh):
    finer = Mesh(
        mesh.devices.reshape(4, 8, 2, mesh.shape["region"]),
        ("member_0", "member_1", "member_2", "region"),
    )
    in_specs = (
        P(MEMBER_REGION, None),
        P("region", MEMBER, None),
        P("region", MEMBER, None),
        P("region", MEMBER, None),
    )
    out_specs = P(MEMBER_REGION, None)
    return jax.shard_map(local, mesh=finer, in_specs=in_specs, out_specs=out_specs, check_vma=False)
```

profile of v0, /device:TPU:1, one launch (start us, length us, event | category | flops | bytes accessed | tf_op | source)
XLA Modules:
  0.0 274.0 jit_solution(13596119832825574276)
XLA Ops:
  0.0 2.6 reshape.100
  2.6 0.1 copy.23
  2.7 2.0 copy.24
  4.7 0.0 copy-start.3
  4.7 15.6 %all-to-all-start = ((bf16[256,2,1024]{2,1,0:T(2,128)(2,1)}), bf16[256,2,1024]{2,1,0:T(2,128)(2,1)S(1)}, u32[]{:S(2)}, u32[]{:S(2)}) async-start(bf16[256,2,1024]{2,1,0:T(2,128)(2,1)} %copy.24), calls=%async_computation | async-start | bytes 2097152 | tf_op jit(solution)/shard_map/all_to_all | solution.py:32
  20.4 0.0 copy-done.3
  20.4 32.4 %all-to-all-done = bf16[256,2,1024]{2,1,0:T(2,128)(2,1)S(1)} async-done(((bf16[256,2,1024]{2,1,0:T(2,128)(2,1)}), bf16[256,2,1024]{2,1,0:T(2,128)(2,1)S(1)}, u32[]{:S(2)}, u32[]{:S(2)}) %all-to-all-start) | async-done | bytes 1048608 | tf_op jit(solution)/shard_map/all_to_all | solution.py:32
  52.8 0.3 copy.25
  53.1 1.1 copy.26
  54.2 0.4 reshape_reshape.9.state
  54.7 0.0 copy-start
  54.7 0.0 copy-start.1
  54.7 0.0 copy-start.2
  54.7 0.5 copy.27
  55.2 0.6 gather_fusion
  55.8 0.0 copy-done
  55.8 0.2 convert_reduce_fusion
  56.0 0.0 copy-done.1
  56.0 0.6 multiply_reduce_fusion
  56.6 0.2 fusion.3
  56.8 0.0 copy-done.2
  56.8 0.2 fusion.1
  57.0 0.7 fusion.10
  57.7 1.1 convolution_bitcast_fusion
  58.8 0.3 copy.32
  59.1 1.8 concatenate.3
  60.9 0.1 pad.4
  61.0 0.8 reshape_reshape.10
  61.8 0.2 copy.28
  62.1 18.8 %all_to_all.35 = f32[8,32,1027]{2,1,0:T(8,128)S(1)} all-to-all(f32[8,32,1027]{2,1,0:T(8,128)S(1)} %copy.28), channel_id=1, replica_groups=mesh['member_0'=4,'member_1'=8,'member_2'=2,'region'=4] {'member_2','reg..., dimensions={0} | all-to-all | bytes 2103296 | tf_op jit(solution)/shard_map/all_to_all | solution.py:39
  80.8 0.1 reduce_sum.58
  80.9 0.1 all_to_all.24
  81.0 12.6 %all_to_all.36 = f32[32,1,1027]{2,1,0:T(1,128)S(1)} all-to-all(f32[32,1,1027]{2,1,0:T(1,128)S(1)} %all_to_all.24), channel_id=1, replica_groups=mesh['member_0'=4,'member_1'=8,'member_2'=2,'region'=4] {'member_0','mem..., dimensions={0} | all-to-all | bytes 262912 | tf_op jit(solution)/shard_map/all_to_all | solution.py:47
  93.6 0.1 reduce_sum.59
  93.7 0.1 broadcast_in_dim.31
  93.8 13.7 %all_to_all.37 = f32[32,1,1027]{2,1,0:T(1,128)S(1)} all-to-all(f32[32,1,1027]{2,1,0:T(1,128)S(1)} %broadcast_in_dim.31), channel_id=1, replica_groups=mesh['member_0'=4,'member_1'=8,'member_2'=2,'region'=4] {'member_0','mem..., dimensions={0} | all-to-all | bytes 262912 | tf_op jit(solution)/shard_map/all_to_all | solution.py:58
  107.5 0.1 broadcast_in_dim.33
  107.5 21.6 %all_to_all.38 = f32[8,32,1027]{2,1,0:T(8,128)S(1)} all-to-all(f32[8,32,1027]{2,1,0:T(8,128)S(1)} %broadcast_in_dim.33), channel_id=1, replica_groups=mesh['member_0'=4,'member_1'=8,'member_2'=2,'region'=4] {'member_2','reg..., dimensions={0} | all-to-all | bytes 2103296 | tf_op jit(solution)/shard_map/all_to_all | solution.py:58
  129.1 0.7 copy.29
  129.8 0.5 reshape_reshape.11
  130.3 0.5 stack.4.sums
  130.9 0.6 slice.19
  131.4 0.1 slice.18
  131.5 1.1 reshape.109.products
  132.6 98.7 %analysis.1 = bf16[512,1024]{1,0:T(8,128)(2,1)} custom-call(f32[512,512]{1,0:T(8,128)} %reshape.109.products, f32[1,512]{1,0:T(1,128)} %bitcast.66, f32[2]{0:T(128)} %stack.4.sums, bf16[512,1024]{1,0:T(8,128)(2,1)} %copy-done), custom_call_target="tpu_custom_call" | custom-call | tf_op jit(solution)/shard_map/analysis/pallas_call | solution.py:267
  231.4 1.5 reshape_reshape_reshape.3
  232.8 37.7 %all_to_all.39 = bf16[256,2,1024]{2,1,0:T(2,128)(2,1)S(1)} all-to-all(bf16[256,2,1024]{2,1,0:T(2,128)(2,1)S(1)} %reshape_reshape_reshape.3), channel_id=1, replica_groups=mesh['member_0'=4,'member_1'=8,'member_2'=2,'region'=4] {'member_0','mem..., dimensions={0} | all-to-all | bytes 2097152 | tf_op jit(solution)/shard_map/all_to_all | solution.py:32
  270.6 0.6 copy.30
  271.1 0.8 reshape.111
  272.0 2.0 copy.33
  (4 shorter events, 0.0 us)
Async XLA Ops:
  4.7 15.7 %copy-start.3 = (s32[1,1,16]{2,1,0:T(1,128)S(1)}, s32[1,1,16]{2,1,0:T(1,128)}, u32[]{:S(2)}) copy-start(s32[1,1,16]{2,1,0:T(1,128)} %param.5) | copy-start | bytes 196
  4.7 48.1 %all-to-all-start = ((bf16[256,2,1024]{2,1,0:T(2,128)(2,1)}), bf16[256,2,1024]{2,1,0:T(2,128)(2,1)S(1)}, u32[]{:S(2)}, u32[]{:S(2)}) async-start(bf16[256,2,1024]{2,1,0:T(2,128)(2,1)} %copy.24), calls=%async_computation | async-start | bytes 2097152 | tf_op jit(solution)/shard_map/all_to_all | solution.py:32
  54.7 1.2 copy-start
  54.7 1.4 copy-start.1
  54.7 2.1 copy-start.2
where the time goes:
time: 274 us
  blocking collectives  104 us (38%)
  Pallas kernels  98.7 us (36%)
  waiting for transfers between devices  32.4 us (12%)
  local copies, waits for them, and re-layouts  19.5 us (7%)
  starting transfers between devices  15.6 us (6%)
    pallas_call x1, Pallas kernels, analysed(): pl.pallas_call(analysis_kernel, name='analysis', out_shape=jax.ShapeDtype...  98.7 us
    all_to_all x1, blocking collectives, one_exchange(): lax.all_to_all(pieces, axis, split_axis=0, concat_axis=0, tiled=True)  37.7 us
    all_to_all x2, blocking collectives, from_everyone(): lax.all_to_all(jnp.broadcast_to(x[None], (devices, *x.shape)), axis, 0, 0...  35.3 us
    all_to_all x1, waiting for transfers between devices, one_exchange(): lax.all_to_all(pieces, axis, split_axis=0, concat_axis=0, tiled=True)  32.4 us
    all_to_all x1, blocking collectives, sent_and_summed(): pieces = lax.all_to_all(split_up(x, dim, devices), axis, 0, 0, tiled=True)  18.8 us
    all_to_all x1, starting transfers between devices, one_exchange(): lax.all_to_all(pieces, axis, split_axis=0, concat_axis=0, tiled=True)  15.6 us
    all_to_all x1, blocking collectives, sum_by_axis(): lax.all_to_all(nearer, far, split_axis=0, concat_axis=0, tiled=True)  12.6 us
  transfers between devices with their start and end apart: 1, of which 1 were waited for; matrix products, arithmetic and copies ran while one was open for 0% of the time, Pallas kernels for 0%

commit v1 on v0

--- a/solution.py
+++ b/solution.py
@@ -11,6 +11,190 @@
 MEMBER_REGION = ("member_0", "member_1", "member_2", "region")
 
 
+MESH_ID = pl.DeviceIdType.MESH
+SIDE_Y, SIDE_Z, CORES, SIDE_X = 4, 8, 2, 4
+
+
+def here():
+    return (
+        lax.axis_index("region"),
+        lax.axis_index("member_0"),
+        lax.axis_index("member_1"),
+        lax.axis_index("member_2"),
+    )
+
+
+def device(x, y, z, c):
+    return (y, z, c, x)
+
+
+def in_plane(i):
+    return lax.rem(i // 4, 4), lax.rem(i // 16, 2), lax.rem(i, 4)
+
+
+PLANE = SIDE_X * SIDE_Y * CORES
+
+
+def plane_peer(i):
+    x, y, z, c = here()
+    dy, dc, dx = in_plane(i)
+    return lax.rem(x + dx, SIDE_X), lax.rem(y + dy, SIDE_Y), z, lax.rem(c + dc, CORES)
+
+
+def line_peer(i):
+    x, y, z, c = here()
+    return x, y, lax.rem(z + i, SIDE_Z), c
+
+
+def greet(barrier):
+    @pl.loop(1, PLANE)
+    def _(i):
+        pl.semaphore_signal(barrier, 1, device_id=device(*plane_peer(i)), device_id_type=MESH_ID)
+
+    @pl.loop(1, SIDE_Z)
+    def _(i):
+        pl.semaphore_signal(barrier, 1, device_id=device(*line_peer(i)), device_id_type=MESH_ID)
+
+
+def met(barrier):
+    pl.semaphore_wait(barrier, PLANE - 1 + SIDE_Z - 1)
+
+
+def remote(src, dst, send, recv, place):
+    return pltpu.make_async_remote_copy(
+        src, dst, send, recv, device_id=device(*place), device_id_type=MESH_ID
+    )
+
+
+def block_of(x, y, z, c):
+    return ((x * SIDE_Y + y) * SIDE_Z + z) * CORES + c
+
+
+def links_of(block, size):
+    return pl.ds(pl.multiple_of(block * size, size), size)
+
+
+def gather_kernel(own, whole, stage, send_p, recv_p, send_z, recv_z):
+    x, y, z, c = here()
+    size = whole.shape[-1]
+    barrier = pltpu.get_barrier_semaphore()
+    greet(barrier)
+    met(barrier)
+
+    @pl.loop(1, PLANE)
+    def _(i):
+        px, py, _, pc = plane_peer(i)
+
+        @pl.loop(0, SIDE_Z)
+        def _(t):
+            remote(
+                own.at[:, links_of(block_of(px, py, t, pc), size)],
+                stage.at[t, y, c * SIDE_X + x],
+                send_p,
+                recv_p,
+                (px, py, z, pc),
+            ).start()
+
+    @pl.loop(0, SIDE_Z)
+    def _(t):
+        stage[t, y, c * SIDE_X + x] = own[:, links_of(block_of(x, y, t, c), size)]
+
+    arrived = own.at[:, pl.ds(0, (PLANE - 1) * SIDE_Z * size)]
+    remote(arrived, arrived, send_p, recv_p, (x, y, z, c)).wait()
+
+    @pl.loop(1, SIDE_Z)
+    def _(i):
+        place = line_peer(i)
+        remote(stage.at[place[2]], whole.at[:, z], send_z, recv_z, place).start()
+
+    whole[:, z] = stage[z]
+    arrived = stage.at[pl.ds(0, SIDE_Z - 1)]
+    remote(arrived, arrived, send_z, recv_z, (x, y, z, c)).wait()
+
+
+def scatter_kernel(whole, own, stage, send_z, recv_z, send_p, recv_p):
+    x, y, z, c = here()
+    size = whole.shape[-1]
+    barrier = pltpu.get_barrier_semaphore()
+    greet(barrier)
+    met(barrier)
+
+    @pl.loop(1, SIDE_Z)
+    def _(i):
+        place = line_peer(i)
+        remote(whole.at[:, place[2]], stage.at[z], send_z, recv_z.at[z], place).start()
+
+    def hand_on(source, block):
+        @pl.loop(1, PLANE)
+        def _(j):
+            px, py, _, pc = plane_peer(j)
+            remote(
+                source.at[py, pc * SIDE_X + px],
+                own.at[:, links_of(block, size)],
+                send_p,
+                recv_p,
+                (px, py, z, pc),
+            ).start()
+
+        own[:, links_of(block, size)] = source[y, c * SIDE_X + x]
+
+    hand_on(whole.at[:, z], block_of(x, y, z, c))
+
+    @pl.loop(1, SIDE_Z)
+    def _(i):
+        t = lax.rem(z + SIDE_Z - i, SIDE_Z)
+        remote(stage.at[t], stage.at[t], send_z, recv_z.at[t], (x, y, z, c)).wait_recv()
+        hand_on(stage.at[t], block_of(x, y, t, c))
+
+    arrived = stage.at[pl.ds(0, SIDE_Z - 1)]
+    remote(arrived, arrived, send_z, recv_z.at[0], (x, y, z, c)).wait_send()
+    arrived = own.at[:, pl.ds(0, (PLANE - 1) * SIDE_Z * size)]
+    remote(arrived, arrived, send_p, recv_p, (x, y, z, c)).wait()
+
+
+VMEM = pl.BlockSpec(memory_space=pltpu.VMEM)
+
+
+def gathered(own):
+    size = own.shape[1] // (PLANE * SIDE_Z)
+    return pl.pallas_call(
+        gather_kernel,
+        name="gather",
+        out_shape=jax.ShapeDtypeStruct(
+            (SIDE_Y, SIDE_Z, CORES * SIDE_X, own.shape[0], size), own.dtype
+        ),
+        in_specs=[VMEM],
+        out_specs=VMEM,
+        scratch_shapes=[
+            pltpu.VMEM((SIDE_Z, SIDE_Y, CORES * SIDE_X, own.shape[0], size), own.dtype),
+            pltpu.SemaphoreType.DMA,
+            pltpu.SemaphoreType.DMA,
+            pltpu.SemaphoreType.DMA,
+            pltpu.SemaphoreType.DMA,
+        ],
+        compiler_params=pltpu.CompilerParams(collective_id=0, has_side_effects=True),
+    )(own)
+
+
+def scattered(whole):
+    rows, size = whole.shape[-2:]
+    return pl.pallas_call(
+        scatter_kernel,
+        name="scatter",
+        out_shape=jax.ShapeDtypeStruct((rows, size * PLANE * SIDE_Z), whole.dtype),
+        in_specs=[VMEM],
+        out_specs=VMEM,
+        scratch_shapes=[
+            pltpu.VMEM((SIDE_Z, SIDE_Y, CORES * SIDE_X, rows, size), whole.dtype),
+            pltpu.SemaphoreType.DMA,
+            pltpu.SemaphoreType.DMA((SIDE_Z,)),
+            pltpu.SemaphoreType.DMA,
+            pltpu.SemaphoreType.DMA,
+        ],
+        compiler_params=pltpu.CompilerParams(collective_id=1, has_side_effects=True),
+    )(whole)
+
+
 def split_up(x, dim, devices):
     dims = x.shape
     pieces = x.reshape(*dims[:dim], devices, dims[dim] // devices, *dims[dim + 1 :])
@@ -21,17 +205,6 @@
     pieces = jnp.moveaxis(pieces, 0, dim)
     dims = pieces.shape
     return pieces.reshape(*dims[:dim], dims[dim] * dims[dim + 1], *dims[dim + 2 :])
-
-
-def one_exchange(x, axis, axes, splits, concats):
-    sizes = [lax.axis_size(a) for a in axes]
-    pieces = split_up(x, splits[0], sizes[0])
-    pieces = jnp.moveaxis(split_up(pieces, splits[1] + 1, sizes[1]), 0, 1)
-    inside = pieces.shape[2:]
-    pieces = pieces.reshape(-1, *inside)
-    pieces = lax.all_to_all(pieces, axis, split_axis=0, concat_axis=0, tiled=True)
-    pieces = laid_out(pieces.reshape(*sizes, *inside), concats[0] + 1)
-    return laid_out(pieces, concats[1])
 
 
 def sent_and_summed(x, axis, dim):
@@ -279,7 +452,7 @@
     regions = lax.axis_size("region")
     own_count = ensemble.shape[0]
     ensemble_size = own_count * members * regions
-    shifted = one_exchange(ensemble, REGION_MEMBER, ("region", MEMBER), (1, 1), (0, 0))
+    shifted = gathered(ensemble).reshape(ensemble_size, -1)
     offsets = obs_offset.reshape(-1)
     values = observed.reshape(-1)
     variance = obs_var.reshape(-1)
@@ -292,7 +465,9 @@
         (products, column, numer, denom), (("member_0", "member_1"), ("member_2", "region"))
     )
     updated = analysed(products, column, numer, denom, shifted)
-    return one_exchange(updated, MEMBER_REGION, (MEMBER, "region"), (0, 0), (1, 1))
+    return scattered(
+        updated.reshape(SIDE_Y, SIDE_Z, CORES * SIDE_X, own_count, updated.shape[1])
+    )
 
 
 def solution(mesh):

time: 274 us -> 278 us (1.015)
  Pallas kernels: 98.7 us -> 188 us
  blocking collectives: 104 us -> 70.5 us
  waiting for transfers between devices: 32.4 us -> 0 us
  starting transfers between devices: 15.6 us -> 0 us
  local copies, waits for them, and re-layouts: 19.5 us -> 14.4 us
    pallas_call x0 -> x2, Pallas kernels: none -> 89.3 us  [the longest x1 52.1 us: gathered(): pl.pallas_call(gather_kernel, name='gather', out_shape=jax.ShapeDtypeStru...]
    all_to_all x1 -> x0, blocking collectives: 37.7 us -> none  [one_exchange(): lax.all_to_all(pieces, axis, split_axis=0, concat_axis=0, tiled=True)]
    all_to_all x1 -> x0, waiting for transfers between devices: 32.4 us -> none  [one_exchange(): lax.all_to_all(pieces, axis, split_axis=0, concat_axis=0, tiled=True)]
    all_to_all x1 -> x0, starting transfers between devices: 15.6 us -> none  [one_exchange(): lax.all_to_all(pieces, axis, split_axis=0, concat_axis=0, tiled=True)]
  transfers between devices with their start and end apart: 1 -> 0, of which waited for: 1 -> 0; matrix products, arithmetic and copies ran while one was open for 0% -> 0% of each run, Pallas kernels for 0% -> 0%
where the time goes in v1:
time: 278 us; the launch traced here: 277 us
  Pallas kernels  188 us (68%)
  blocking collectives  70.5 us (25%)
  local copies, waits for them, and re-layouts  14.4 us (5%)
  other arithmetic  3.17 us (1%)
    pallas_call x1, Pallas kernels, analysed(): pl.pallas_call(analysis_kernel, name='analysis', out_shape=jax.ShapeDtype...  98.3 us
    pallas_call x1, Pallas kernels, gathered(): pl.pallas_call(gather_kernel, name='gather', out_shape=jax.ShapeDtypeStru...  52.1 us
    pallas_call x1, Pallas kernels, scattered(): pl.pallas_call(scatter_kernel, name='scatter', out_shape=jax.ShapeDtypeSt...  37.2 us
    all_to_all x2, blocking collectives, from_everyone(): lax.all_to_all(jnp.broadcast_to(x[None], (devices, *x.shape)), axis, 0, 0...  35.3 us
    all_to_all x1, blocking collectives, sent_and_summed(): pieces = lax.all_to_all(split_up(x, dim, devices), axis, 0, 0, tiled=True)  20.3 us
    all_to_all x1, blocking collectives, sum_by_axis(): lax.all_to_all(nearer, far, split_axis=0, concat_axis=0, tiled=True)  14.9 us

profile of v1, /device:TPU:1, one launch (start us, length us, event | category | flops | bytes accessed | tf_op | source)
XLA Modules:
  0.0 277.1 jit_solution(17688371633230041497)
XLA Ops:
  0.0 0.7 compare_and_fusion
  0.7 0.7 fusion.7
  1.3 52.1 %gather.8 = bf16[4,8,8,2,1024]{4,3,2,1,0:T(2,128)(2,1)} custom-call(bf16[2,262144]{1,0:T(2,128)(2,1)} %own.1), custom_call_target="tpu_custom_call" | custom-call | tf_op jit(solution)/shard_map/gather/pallas_call | solution.py:160
  53.5 1.5 reshape.84.state
  54.9 0.0 copy-start
  54.9 0.0 copy-start.1
  55.0 0.0 copy-start.2
  55.0 0.5 copy.9
  55.5 0.6 gather_fusion
  56.1 0.0 copy-done
  56.1 0.2 convert_reduce_fusion
  56.3 0.0 copy-done.1
  56.3 0.6 multiply_reduce_fusion
  56.9 0.2 fusion.3
  57.1 0.0 copy-done.2
  57.1 0.2 fusion.1
  57.3 0.7 fusion.10
  58.0 1.1 convolution_bitcast_fusion
  59.1 0.3 copy.13
  59.4 1.8 concatenate.3
  61.2 0.1 pad.4
  61.3 0.8 reshape_reshape.6
  62.1 0.2 copy.10
  62.3 20.3 %all_to_all.25 = f32[8,32,1027]{2,1,0:T(8,128)S(1)} all-to-all(f32[8,32,1027]{2,1,0:T(8,128)S(1)} %copy.10), channel_id=1, replica_groups=mesh['member_0'=4,'member_1'=8,'member_2'=2,'region'=4] {'member_2','reg..., dimensions={0} | all-to-all | bytes 2103296 | tf_op jit(solution)/shard_map/all_to_all | solution.py:212
  82.6 0.1 reduce_sum.58
  82.7 0.1 all_to_all.17
  82.8 14.9 %all_to_all.26 = f32[32,1,1027]{2,1,0:T(1,128)S(1)} all-to-all(f32[32,1,1027]{2,1,0:T(1,128)S(1)} %all_to_all.17), channel_id=1, replica_groups=mesh['member_0'=4,'member_1'=8,'member_2'=2,'region'=4] {'member_0','mem..., dimensions={0} | all-to-all | bytes 262912 | tf_op jit(solution)/shard_map/all_to_all | solution.py:220
  97.7 0.1 reduce_sum.59
  97.8 0.1 broadcast_in_dim.31
  97.9 13.7 %all_to_all.27 = f32[32,1,1027]{2,1,0:T(1,128)S(1)} all-to-all(f32[32,1,1027]{2,1,0:T(1,128)S(1)} %broadcast_in_dim.31), channel_id=1, replica_groups=mesh['member_0'=4,'member_1'=8,'member_2'=2,'region'=4] {'member_0','mem..., dimensions={0} | all-to-all | bytes 262912 | tf_op jit(solution)/shard_map/all_to_all | solution.py:231
  111.6 0.1 broadcast_in_dim.33
  111.7 21.6 %all_to_all.28 = f32[8,32,1027]{2,1,0:T(8,128)S(1)} all-to-all(f32[8,32,1027]{2,1,0:T(8,128)S(1)} %broadcast_in_dim.33), channel_id=1, replica_groups=mesh['member_0'=4,'member_1'=8,'member_2'=2,'region'=4] {'member_2','reg..., dimensions={0} | all-to-all | bytes 2103296 | tf_op jit(solution)/shard_map/all_to_all | solution.py:231
  133.3 0.7 copy.11
  134.0 0.5 reshape_reshape.7
  134.5 0.5 stack.4.sums
  135.0 0.6 slice.19
  135.6 0.1 slice.18
  135.7 1.1 reshape.91.products
  136.8 98.3 %analysis.1 = bf16[512,1024]{1,0:T(8,128)(2,1)} custom-call(f32[512,512]{1,0:T(8,128)} %reshape.91.products, f32[1,512]{1,0:T(1,128)} %bitcast.42, f32[2]{0:T(128)} %stack.4.sums, bf16[512,1024]{1,0:T(8,128)(2,1)} %copy-done), custom_call_target="tpu_custom_call" | custom-call | tf_op jit(solution)/shard_map/analysis/pallas_call | solution.py:440
  235.1 2.2 reshape.92.whole
  237.4 37.2 %scatter.1 = bf16[2,262144]{1,0:T(2,128)(2,1)} custom-call(bf16[4,8,8,2,1024]{4,3,2,1,0:T(2,128)(2,1)} %reshape.92.whole), custom_call_target="tpu_custom_call" | custom-call | tf_op jit(solution)/shard_map/scatter/pallas_call | solution.py:181
  274.5 2.6 copy.17
  (2 shorter events, 0.0 us)
Async XLA Ops:
  54.9 1.2 copy-start
  54.9 1.4 copy-start.1
  55.0 2.1 copy-start.2

commit v2 on v1

--- a/solution.py
+++ b/solution.py
@@ -7,7 +7,6 @@
 from jax.sharding import PartitionSpec as P
 
 MEMBER = ("member_0", "member_1", "member_2")
-REGION_MEMBER = ("region", "member_0", "member_1", "member_2")
 MEMBER_REGION = ("member_0", "member_1", "member_2", "region")
 
 
@@ -28,6 +27,11 @@
     return (y, z, c, x)
 
 
+def chip_peer(i):
+    x, y, z, c = here()
+    return lax.rem(x + i, SIDE_X), lax.rem(y + i // SIDE_X, SIDE_Y), z, c
+
+
 def in_plane(i):
     return lax.rem(i // 4, 4), lax.rem(i // 16, 2), lax.rem(i, 4)
 
@@ -74,12 +78,35 @@
     return pl.ds(pl.multiple_of(block * size, size), size)
 
 
-def gather_kernel(own, whole, stage, send_p, recv_p, send_z, recv_z):
+def no_matter(ref, send, recv):
+    return remote(ref, ref, send, recv, here())
+
+
+def dot6_t(a, b):
+    return lax.dot_general(
+        a,
+        b,
+        (((1,), (1,)), ((), ())),
+        precision=lax.Precision.HIGHEST,
+        preferred_element_type=jnp.float32,
+    )
+
+
+def gather_kernel(
+    own, notes, whole, total, sums,
+    pieces, stage, all_notes, seen, picked, product, half, chunks, extras, other, send, recv,
+):
     x, y, z, c = here()
-    size = whole.shape[-1]
+    size = own.shape[1] // (PLANE * SIDE_Z)
+    members = total.shape[0]
+    seat = c * SIDE_X + x
     barrier = pltpu.get_barrier_semaphore()
     greet(barrier)
     met(barrier)
+
+    @pl.loop(1, SIDE_Z)
+    def _(i):
+        remote(notes, all_notes.at[z], send.at[0], recv.at[0], line_peer(i)).start()
 
     @pl.loop(1, PLANE)
     def _(i):
@@ -89,34 +116,135 @@
         def _(t):
             remote(
                 own.at[:, links_of(block_of(px, py, t, pc), size)],
-                stage.at[t, y, c * SIDE_X + x],
-                send_p,
-                recv_p,
+                pieces.at[t, y, seat],
+                send.at[1],
+                recv.at[1],
                 (px, py, z, pc),
             ).start()
 
+    all_notes[z] = notes[...]
+
     @pl.loop(0, SIDE_Z)
     def _(t):
-        stage[t, y, c * SIDE_X + x] = own[:, links_of(block_of(x, y, t, c), size)]
-
-    arrived = own.at[:, pl.ds(0, (PLANE - 1) * SIDE_Z * size)]
-    remote(arrived, arrived, send_p, recv_p, (x, y, z, c)).wait()
+        pieces[t, y, seat] = own[:, links_of(block_of(x, y, t, c), size)]
+
+    no_matter(all_notes.at[pl.ds(0, SIDE_Z - 1)], send.at[0], recv.at[0]).wait()
+    table = jnp.sum(all_notes[...], axis=0)
+    offset = table[0:1, :].astype(jnp.int32)
+    measured = table[1:2, :]
+    variance = table[2:3, :]
+    watches = table.shape[1]
+    link = lax.broadcasted_iota(jnp.int32, (size, watches), 0)
+    seen[...] = jnp.where(link == offset, 1.0, 0.0).astype(jnp.bfloat16)
+
+    no_matter(own.at[:, pl.ds(0, (PLANE - 1) * SIDE_Z * size)], send.at[1], recv.at[1]).wait()
+    line = lax.broadcasted_iota(jnp.int32, (members // SIDE_Z, watches), 1) // (watches // SIDE_Z)
+
+    def pick(t, found):
+        def lay(k, _):
+            stage[t, k] = pieces[t, k].reshape(stage.shape[2:])
+            return 0
+
+        lax.fori_loop(0, SIDE_Y, lay, 0)
+        rows = stage[t].reshape(members // SIDE_Z, size)
+        values = jnp.dot(rows, seen[...], preferred_element_type=jnp.float32)
+        return jnp.where(line == t, values, found)
+
+    found = lax.fori_loop(0, SIDE_Z, pick, jnp.zeros(line.shape, jnp.float32))
+    mine = picked.at[SIDE_Z]
+    mine[...] = found.astype(jnp.bfloat16).reshape(mine.shape)
 
     @pl.loop(1, SIDE_Z)
     def _(i):
+        remote(mine, picked.at[z], send.at[2], recv.at[2], line_peer(i)).start()
+
+    @pl.loop(1, SIDE_Z)
+    def _(i):
         place = line_peer(i)
-        remote(stage.at[place[2]], whole.at[:, z], send_z, recv_z, place).start()
-
+        remote(stage.at[place[2]], whole.at[:, z], send.at[3], recv.at[3], place).start()
+
+    picked[z] = mine[...]
     whole[:, z] = stage[z]
-    arrived = stage.at[pl.ds(0, SIDE_Z - 1)]
-    remote(arrived, arrived, send_z, recv_z, (x, y, z, c)).wait()
-
-
-def scatter_kernel(whole, own, stage, send_z, recv_z, send_p, recv_p):
+    no_matter(picked.at[pl.ds(0, SIDE_Z - 1)], send.at[2], recv.at[2]).wait()
+
+    values = jnp.swapaxes(picked[pl.ds(0, SIDE_Z)], 0, 1).reshape(members, watches)
+    values = values.astype(jnp.float32)
+    center = jnp.sum(values, axis=0, keepdims=True) * (1.0 / members)
+    anomaly = values - center
+    innovation = measured - center
+    weight = 1.0 / ((members - 1.0) * variance)
+    spread = jnp.sum(anomaly * anomaly, axis=0, keepdims=True) * (1.0 / (members - 1.0)) + variance
+    column = dot6_t(weight * innovation, anomaly)
+    numer = jnp.sum(innovation * innovation, axis=1, keepdims=True)
+    denom = jnp.sum(spread, axis=1, keepdims=True)
+    lane = lax.broadcasted_iota(jnp.int32, column.shape, 1)
+    extra = extras.at[PLANE]
+    extra[0:1, :] = column
+    extra[1:2, :] = jnp.where(lane == 0, numer, jnp.where(lane == 1, denom, 0.0))
+    product[...] = dot6_t(anomaly * weight, anomaly)
+
+    rows = members // CORES
+    kept = pl.ds(pl.multiple_of(c * rows, rows), rows)
+    given = pl.ds(pl.multiple_of((1 - c) * rows, rows), rows)
+    partner = (x, y, z, 1 - c)
+    remote(product.at[given], other, send.at[4], recv.at[4], partner).start()
+
+    @pl.loop(1, PLANE)
+    def _(i):
+        remote(
+            extra, extras.at[y * (CORES * SIDE_X) + seat], send.at[5], recv.at[5], plane_peer(i)
+        ).start()
+
+    extras[y * (CORES * SIDE_X) + seat] = extra[...]
+    no_matter(other, send.at[4], recv.at[4]).wait()
+    half[...] = product[kept, :] + other[...]
+    chips = SIDE_X * SIDE_Y
+    part = rows // chips
+
+    def part_of(px, py, base=0):
+        return pl.ds(pl.multiple_of(base + (py * SIDE_X + px) * part, part), part)
+
+    @pl.loop(1, chips)
+    def _(i):
+        place = chip_peer(i)
+        remote(
+            half.at[part_of(place[0], place[1])],
+            chunks.at[y * SIDE_X + x],
+            send.at[6],
+            recv.at[6],
+            place,
+        ).start()
+
+    chunks[y * SIDE_X + x] = half[part_of(x, y), :]
+    no_matter(chunks.at[pl.ds(0, chips - 1)], send.at[6], recv.at[6]).wait()
+    done = total.at[part_of(x, y, c * rows)]
+    done[...] = jnp.sum(chunks[...], axis=0)
+
+    @pl.loop(1, chips)
+    def _(i):
+        remote(done, done, send.at[7], recv.at[7], chip_peer(i)).start()
+
+    no_matter(half.at[pl.ds(0, rows - part)], send.at[7], recv.at[7]).wait()
+    remote(total.at[kept], total.at[kept], send.at[8], recv.at[8], partner).start()
+    no_matter(extras.at[pl.ds(0, PLANE - 1)], send.at[5], recv.at[5]).wait()
+    sums[...] = jnp.sum(extras[pl.ds(0, PLANE)], axis=0)
+    no_matter(other, send.at[8], recv.at[8]).wait()
+    no_matter(stage.at[pl.ds(0, SIDE_Z - 1)], send.at[3], recv.at[3]).wait()
+
+
+def scatter_kernel(high, low, state, own, whole, stage, send_z, recv_z, send_p, recv_p):
     x, y, z, c = here()
-    size = whole.shape[-1]
+    rows, size = state.shape
     barrier = pltpu.get_barrier_semaphore()
     greet(barrier)
+    wide = 256
+
+    @pl.loop(0, size // wide)
+    def _(k):
+        at = links_of(k, wide)
+        values = dot1(high[...], state[:, at]) + dot1(low[...], state[:, at])
+        whole[:, :, :, :, at] = values.astype(jnp.bfloat16).reshape(*whole.shape[:-1], wide)
+
     met(barrier)
 
     @pl.loop(1, SIDE_Z)
@@ -155,118 +283,60 @@
 VMEM = pl.BlockSpec(memory_space=pltpu.VMEM)
 
 
-def gathered(own):
+def gathered(own, notes, members):
     size = own.shape[1] // (PLANE * SIDE_Z)
+    seats = CORES * SIDE_X
+    rows = own.shape[0]
+    watches = notes.shape[1]
+    part = (members // CORES) // (SIDE_X * SIDE_Y)
+    f32, bf16 = jnp.float32, jnp.bfloat16
     return pl.pallas_call(
         gather_kernel,
         name="gather",
-        out_shape=jax.ShapeDtypeStruct(
-            (SIDE_Y, SIDE_Z, CORES * SIDE_X, own.shape[0], size), own.dtype
+        out_shape=(
+            jax.ShapeDtypeStruct((SIDE_Y, SIDE_Z, seats * rows, size), bf16),
+            jax.ShapeDtypeStruct((members, members), f32),
+            jax.ShapeDtypeStruct((2, members), f32),
         ),
-        in_specs=[VMEM],
-        out_specs=VMEM,
+        in_specs=[VMEM, VMEM],
+        out_specs=(VMEM, VMEM, VMEM),
         scratch_shapes=[
-            pltpu.VMEM((SIDE_Z, SIDE_Y, CORES * SIDE_X, own.shape[0], size), own.dtype),
-            pltpu.SemaphoreType.DMA,
-            pltpu.SemaphoreType.DMA,
-            pltpu.SemaphoreType.DMA,
-            pltpu.SemaphoreType.DMA,
+            pltpu.VMEM((SIDE_Z, SIDE_Y, seats, rows, size), bf16),
+            pltpu.VMEM((SIDE_Z, SIDE_Y, seats * rows, size), bf16),
+            pltpu.VMEM((SIDE_Z, *notes.shape), f32),
+            pltpu.VMEM((size, watches), bf16),
+            pltpu.VMEM((SIDE_Z + 1, SIDE_Y, seats * rows, watches), bf16),
+            pltpu.VMEM((members, members), f32),
+            pltpu.VMEM((members // CORES, members), f32),
+            pltpu.VMEM((SIDE_X * SIDE_Y, part, members), f32),
+            pltpu.VMEM((PLANE + 1, 2, members), f32),
+            pltpu.VMEM((members // CORES, members), f32),
+            pltpu.SemaphoreType.DMA((9,)),
+            pltpu.SemaphoreType.DMA((9,)),
         ],
         compiler_params=pltpu.CompilerParams(collective_id=0, has_side_effects=True),
-    )(own)
-
-
-def scattered(whole):
-    rows, size = whole.shape[-2:]
+    )(own, notes)
+
+
+def scattered(high, low, state, own_rows):
+    rows, size = state.shape
+    shape = (SIDE_Y, SIDE_Z, CORES * SIDE_X, own_rows, size)
     return pl.pallas_call(
         scatter_kernel,
         name="scatter",
-        out_shape=jax.ShapeDtypeStruct((rows, size * PLANE * SIDE_Z), whole.dtype),
-        in_specs=[VMEM],
+        out_shape=jax.ShapeDtypeStruct((own_rows, size * PLANE * SIDE_Z), state.dtype),
+        in_specs=[VMEM, VMEM, VMEM],
         out_specs=VMEM,
         scratch_shapes=[
-            pltpu.VMEM((SIDE_Z, SIDE_Y, CORES * SIDE_X, rows, size), whole.dtype),
+            pltpu.VMEM(shape, state.dtype),
+            pltpu.VMEM((SIDE_Z, SIDE_Y, *shape[2:]), state.dtype),
             pltpu.SemaphoreType.DMA,
             pltpu.SemaphoreType.DMA((SIDE_Z,)),
             pltpu.SemaphoreType.DMA,
             pltpu.SemaphoreType.DMA,
         ],
         compiler_params=pltpu.CompilerParams(collective_id=1, has_side_effects=True),
-    )(whole)
-
-
-def split_up(x, dim, devices):
-    dims = x.shape
-    pieces = x.reshape(*dims[:dim], devices, dims[dim] // devices, *dims[dim + 1 :])
-    return jnp.moveaxis(pieces, dim, 0)
-
-
-def laid_out(pieces, dim):
-    pieces = jnp.moveaxis(pieces, 0, dim)
-    dims = pieces.shape
-    return pieces.reshape(*dims[:dim], dims[dim] * dims[dim + 1], *dims[dim + 2 :])
-
-
-def sent_and_summed(x, axis, dim):
-    devices = lax.axis_size(axis)
-    pieces = lax.all_to_all(split_up(x, dim, devices), axis, 0, 0, tiled=True)
-    return jnp.sum(pieces, axis=0)
-
-
-def sum_by_axis(x, axes, dim):
-    far, near = axes
-    pieces = split_up(x, dim, lax.axis_size(far))
-    nearer = sent_and_summed(pieces, near, dim + 1)
-    arrived = lax.all_to_all(nearer, far, split_axis=0, concat_axis=0, tiled=True)
-    return arrived.sum(axis=0)
-
-
-def rows_for(lines, devices):
-    spare = -len(lines) % devices
-    return jnp.pad(lines, [(0, spare)] + [(0, 0)] * (lines.ndim - 1))
-
-
-def from_everyone(x, axis):
-    devices = lax.axis_size(axis)
-    return lax.all_to_all(jnp.broadcast_to(x[None], (devices, *x.shape)), axis, 0, 0, tiled=True)
-
-
-def whole_of(x, axes, dim):
-    far, near = axes
-    first = from_everyone(x, far)
-    pieces = jnp.swapaxes(from_everyone(first, near), 0, 1)
-    return laid_out(pieces.reshape(-1, *x.shape), dim)
-
-
-def sum_by_parts(x, axes):
-    own = sum_by_axis(rows_for(x, lax.axis_size(axes[0]) * lax.axis_size(axes[1])), axes, 0)
-    whole = whole_of(own, axes, 0)
-    return whole[: len(x)].reshape(x.shape)
-
-
-def together(arrays, axis):
-    ends = [0]
-    for a in arrays:
-        ends.append(ends[-1] + a.size)
-    total = sum_by_parts(jnp.concatenate([a.ravel() for a in arrays]), axis)
-    return tuple((total[b:e].reshape(a.shape) for a, b, e in zip(arrays, ends, ends[1:])))
-
-
-def observation_terms(picked, values, variance, ensemble_size):
-    center = jnp.mean(picked, axis=1, keepdims=True)
-    anomaly = picked - center
-    innovation = values - center[:, 0]
-    numer = jnp.sum(innovation * innovation)
-    denom = jnp.sum(jnp.sum(anomaly * anomaly, axis=1) / (ensemble_size - 1.0) + variance)
-    weight = 1.0 / ((ensemble_size - 1.0) * variance)
-    return (anomaly, innovation, weight, numer, denom)
-
-
-def weighted_products(anomaly, innovation, weight):
-    weighted = anomaly * weight[:, None]
-    products = jnp.dot(weighted.T, anomaly, precision=lax.Precision.HIGHEST)
-    column = jnp.dot(innovation * weight, anomaly, precision=lax.Precision.HIGHEST)
-    return (products, column)
+    )(high, low, state)
 
 
 def split_bf16(a):
@@ -399,9 +469,9 @@
         newton(dot6, dot6)
 
 
-def analysis_kernel(products, column, sums, state, out, x, system, r, tmp):
+def mixing_kernel(products, sums, high, low, x, system, r, tmp):
     n = products.shape[0]
-    square = sums[0] / sums[1]
+    square = jnp.sum(sums[1:2, 0:1] / sums[1:2, 1:2])
     inflation = jnp.sqrt(jnp.full((1, n), square, jnp.float32))
 
     def scaled(rows, trace):
@@ -420,54 +490,43 @@
     by_rows(n, shifted, 0)
     inverse_into(x, system, r, tmp)
 
-    q = dot6(column[...], x[...])
+    q = dot6(sums[0:1, :], x[...])
 
     def mix(rows, _):
         eye = unit(rows, n)
         mixing = 0.5 * inflation * (eye + x[rows, :]) + square * q
         mean = jnp.sum(mixing, axis=1, keepdims=True) * (1.0 / n)
-        high, low = split_bf16(mixing - mean + 1.0 / n)
-        out[rows, :] = (dot1(high, state[...]) + dot1(low, state[...])).astype(jnp.bfloat16)
+        high[rows, :], low[rows, :] = split_bf16(mixing - mean + 1.0 / n)
         return 0
 
     by_rows(n, mix, 0)
 
 
-def analysed(products, column, numer, denom, state):
+def mixed(products, sums):
     n = products.shape[0]
-    sums = jnp.stack([numer, denom])
-    vmem = pl.BlockSpec(memory_space=pltpu.VMEM)
     return pl.pallas_call(
-        analysis_kernel,
-        name="analysis",
-        out_shape=jax.ShapeDtypeStruct(state.shape, jnp.bfloat16),
-        in_specs=[vmem, vmem, pl.BlockSpec(memory_space=pltpu.SMEM), vmem],
-        out_specs=vmem,
+        mixing_kernel,
+        name="mixing",
+        out_shape=[jax.ShapeDtypeStruct((n, n), jnp.bfloat16)] * 2,
+        in_specs=[VMEM, VMEM],
+        out_specs=[VMEM, VMEM],
         scratch_shapes=[pltpu.VMEM((n, n), jnp.float32) for _ in range(4)],
-    )(products, column[None, :], sums, state)
+    )(products, sums)
 
 
 def local(ensemble, obs_offset, observed, obs_var):
-    members = lax.axis_size(MEMBER)
-    regions = lax.axis_size("region")
-    own_count = ensemble.shape[0]
-    ensemble_size = own_count * members * regions
-    shifted = gathered(ensemble).reshape(ensemble_size, -1)
-    offsets = obs_offset.reshape(-1)
-    values = observed.reshape(-1)
-    variance = obs_var.reshape(-1)
-    picked = jnp.take(shifted, offsets, axis=1).T.astype(jnp.float32)
-    anomaly, innovation, weight, numer, denom = observation_terms(
-        picked, values, variance, ensemble_size
-    )
-    products, column = weighted_products(anomaly, innovation, weight)
-    products, column, numer, denom = together(
-        (products, column, numer, denom), (("member_0", "member_1"), ("member_2", "region"))
-    )
-    updated = analysed(products, column, numer, denom, shifted)
-    return scattered(
-        updated.reshape(SIDE_Y, SIDE_Z, CORES * SIDE_X, own_count, updated.shape[1])
-    )
+    own_rows = ensemble.shape[0]
+    members = own_rows * PLANE * SIDE_Z
+    count = obs_offset.size
+    notes = jnp.concatenate(
+        [obs_offset.astype(jnp.float32).reshape(1, -1), observed.reshape(1, -1), obs_var.reshape(1, -1)]
+    )
+    notes = jnp.pad(notes, ((0, 5), (0, 0)))
+    seat = lax.broadcasted_iota(jnp.int32, (8, SIDE_Z * count), 1) // count
+    notes = jnp.where(seat == lax.axis_index("member_1"), jnp.tile(notes, (1, SIDE_Z)), 0.0)
+    state, products, sums = gathered(ensemble, notes, members)
+    high, low = mixed(products, sums)
+    return scattered(high, low, state.reshape(members, -1), own_rows)
 
 
 def solution(mesh):

time: 278 us -> 210 us (0.76)
  blocking collectives: 70.5 us -> 0 us
  Pallas kernels: 188 us -> 205 us
  local copies, waits for them, and re-layouts: 14.4 us -> 3.97 us
    all_to_all x4 -> x0, blocking collectives: 70.5 us -> none  [the longest x2 35.3 us: from_everyone(): lax.all_to_all(jnp.broadcast_to(x[None], (devices, *x.shape)), axis, 0, 0...]
    pallas_call x1, Pallas kernels: 37.2 us -> 48.2 us  [scattered(): pl.pallas_call(scatter_kernel, name='scatter', out_shape=jax.ShapeDtypeSt...]
    pallas_call x2, Pallas kernels: 150 us -> 157 us  [the longest x1 96.2 us: mixed(): pl.pallas_call(mixing_kernel, name='mixing', out_shape=[jax.ShapeDtypeStr...]
    reshape x4 -> x0, local copies, waits for them, and re-layouts: 5.39 us -> none  [the longest x1 2.25 us: local(): updated.reshape(SIDE_Y, SIDE_Z, CORES * SIDE_X, own_count, updated.shape[1])]
where the time goes in v2:
time: 210 us
  Pallas kernels  205 us (98%)
  local copies, waits for them, and re-layouts  3.97 us (2%)
    pallas_call x1, Pallas kernels, mixed(): pl.pallas_call(mixing_kernel, name='mixing', out_shape=[jax.ShapeDtypeStr...  96.2 us
    pallas_call x1, Pallas kernels, gathered(): pl.pallas_call(gather_kernel, name='gather', out_shape=(jax.ShapeDtypeStr...  60.5 us
    pallas_call x1, Pallas kernels, scattered(): pl.pallas_call(scatter_kernel, name='scatter', out_shape=jax.ShapeDtypeSt...  48.2 us

profile of v2, /device:TPU:1, one launch (start us, length us, event | category | flops | bytes accessed | tf_op | source)
XLA Modules:
  0.0 209.6 jit_solution(9556340957954038437)
XLA Ops:
  0.0 0.0 copy-start.2
  0.0 0.7 copy-done.2
  0.7 0.0 copy-start
  0.7 0.0 copy-start.1
  0.7 0.6 copy-done
  1.3 0.0 copy-done.1
  1.4 0.1 tile.10
  1.5 0.6 fusion.notes
  2.1 60.5 %gather.1 = (bf16[4,8,16,1024]{3,2,1,0:T(8,128)(2,1)}, f32[512,512]{1,0:T(8,128)}, f32[2,512]{1,0:T(2,128)}) custom-call(bf16[2,262144]{1,0:T(2,128)(2,1)} %own.1, f32[8,128]{1,0:T(8,128)} %fusion.notes), custom_call_target="tpu_custom_call" | custom-call | tf_op jit(solution)/shard_map/gather/pallas_call | solution.py:293
  62.6 96.2 %mixing.1 = (bf16[512,512]{1,0:T(8,128)(2,1)}, bf16[512,512]{1,0:T(8,128)(2,1)}) custom-call(f32[512,512]{1,0:T(8,128)} %get-tuple-element.10.products, f32[2,512]{1,0:T(2,128)} %get-tuple-element.11.sums), custom_call_target="tpu_custom_call" | custom-call | tf_op jit(solution)/shard_map/mixing/pallas_call | solution.py:507
  158.8 48.2 %scatter.1 = bf16[2,262144]{1,0:T(2,128)(2,1)} custom-call(bf16[512,512]{1,0:T(8,128)(2,1)} %get-tuple-element.12.high, bf16[512,512]{1,0:T(8,128)(2,1)} %get-tuple-element.13.low, bf16[512,1024]{1,0:T(8,128)(2,1)} %bitcast.5), custom_call_target="tpu_custom_call" | custom-call | tf_op jit(solution)/shard_map/scatter/pallas_call | solution.py:324
  207.0 2.6 %copy.6 = bf16[2,262144]{1,0:T(2,128)(2,1)} copy(bf16[2,262144]{1,0:T(2,128)(2,1)} %scatter.1) | data formatting | bytes 2097152
  (5 shorter events, 0.0 us)
Async XLA Ops:
  0.0 0.7 copy-start.2
  0.7 0.7 copy-start
  0.7 0.7 copy-start.1

commit v3 on v2

--- a/solution.py
+++ b/solution.py
@@ -92,62 +92,103 @@
     )
 
 
+def along(k):
+    d = k // 2 + 1
+    return lax.rem(jnp.where(lax.rem(k, 2) == 0, d, SIDE_Z - d), SIDE_Z) * jnp.where(k == 7, 0, 1)
+
+
+EARLY = 4
+
+
 def gather_kernel(
-    own, notes, whole, total, sums,
-    pieces, stage, all_notes, seen, picked, product, half, chunks, extras, other, send, recv,
+    ensemble, offsets, observed, variances, whole, total, sums,
+    own, notes, numbers, pieces, stage, all_notes, seen, picked, product, half, chunks, extras,
+    other, copied, send, recv, arrived,
 ):
     x, y, z, c = here()
     size = own.shape[1] // (PLANE * SIDE_Z)
     members = total.shape[0]
     seat = c * SIDE_X + x
+    loads = [
+        pltpu.make_async_copy(ensemble, own, copied.at[0]),
+        pltpu.make_async_copy(offsets.at[0], numbers, copied.at[1]),
+        pltpu.make_async_copy(observed.at[0], notes.at[pl.ds(1, 1), :], copied.at[2]),
+        pltpu.make_async_copy(variances.at[0], notes.at[pl.ds(2, 1), :], copied.at[3]),
+    ]
+    for load in loads:
+        load.start()
     barrier = pltpu.get_barrier_semaphore()
     greet(barrier)
+    for load in loads:
+        load.wait()
+    notes[0:1, :] = numbers[...].astype(jnp.float32)
+    count, watches = notes.shape[1], all_notes.shape[2]
+    to = lax.broadcasted_iota(jnp.int32, (count, watches), 1)
+    at = lax.broadcasted_iota(jnp.int32, (count, watches), 0) + z * count
+    row = lax.broadcasted_iota(jnp.int32, (8, count), 0)
+    placed = dot6(
+        jnp.where(row < 3, notes[...], 0.0), jnp.where(to == at, 1.0, 0.0).astype(jnp.float32)
+    )
+    mine = all_notes.at[SIDE_Z]
+    mine[...] = placed
+
+    @pl.loop(0, SIDE_Z)
+    def _(t):
+        pieces[t, y, seat] = own[:, links_of(block_of(x, y, t, c), size)]
+
     met(barrier)
 
     @pl.loop(1, SIDE_Z)
     def _(i):
-        remote(notes, all_notes.at[z], send.at[0], recv.at[0], line_peer(i)).start()
-
-    @pl.loop(1, PLANE)
-    def _(i):
-        px, py, _, pc = plane_peer(i)
-
-        @pl.loop(0, SIDE_Z)
-        def _(t):
+        remote(mine, all_notes.at[z], send.at[0], recv.at[0], line_peer(i)).start()
+
+    @pl.loop(0, SIDE_Z)
+    def _(k):
+        t = lax.rem(z + along(k), SIDE_Z)
+
+        @pl.loop(1, PLANE)
+        def _(i):
+            px, py, _, pc = plane_peer(i)
             remote(
                 own.at[:, links_of(block_of(px, py, t, pc), size)],
                 pieces.at[t, y, seat],
                 send.at[1],
-                recv.at[1],
+                arrived.at[t],
                 (px, py, z, pc),
             ).start()
 
-    all_notes[z] = notes[...]
-
-    @pl.loop(0, SIDE_Z)
-    def _(t):
-        pieces[t, y, seat] = own[:, links_of(block_of(x, y, t, c), size)]
-
+    all_notes[z] = placed
     no_matter(all_notes.at[pl.ds(0, SIDE_Z - 1)], send.at[0], recv.at[0]).wait()
-    table = jnp.sum(all_notes[...], axis=0)
+    table = jnp.sum(all_notes[pl.ds(0, SIDE_Z)], axis=0)
     offset = table[0:1, :].astype(jnp.int32)
     measured = table[1:2, :]
     variance = table[2:3, :]
-    watches = table.shape[1]
     link = lax.broadcasted_iota(jnp.int32, (size, watches), 0)
     seen[...] = jnp.where(link == offset, 1.0, 0.0).astype(jnp.bfloat16)
-
-    no_matter(own.at[:, pl.ds(0, (PLANE - 1) * SIDE_Z * size)], send.at[1], recv.at[1]).wait()
-    line = lax.broadcasted_iota(jnp.int32, (members // SIDE_Z, watches), 1) // (watches // SIDE_Z)
-
-    def pick(t, found):
-        def lay(k, _):
-            stage[t, k] = pieces[t, k].reshape(stage.shape[2:])
+    line = lax.broadcasted_iota(jnp.int32, (members // SIDE_Z, watches), 1) // count
+
+    def pass_on(k):
+        t = lax.rem(z + along(k), SIDE_Z)
+        remote(stage.at[t], whole.at[:, z], send.at[3], recv.at[3], (x, y, t, c)).start()
+
+    def pick(k, found):
+        t = lax.rem(z + along(k), SIDE_Z)
+        no_matter(
+            own.at[:, pl.ds(0, (PLANE - 1) * size)], send.at[1], arrived.at[t]
+        ).wait_recv()
+
+        def lay(j, _):
+            stage[t, j] = pieces[t, j].reshape(stage.shape[2:])
             return 0
 
         lax.fori_loop(0, SIDE_Y, lay, 0)
         rows = stage[t].reshape(members // SIDE_Z, size)
         values = jnp.dot(rows, seen[...], preferred_element_type=jnp.float32)
+
+        @pl.when(jnp.logical_and(k >= 1, k <= EARLY))
+        def _():
+            pass_on(k - 1)
+
         return jnp.where(line == t, values, found)
 
     found = lax.fori_loop(0, SIDE_Z, pick, jnp.zeros(line.shape, jnp.float32))
@@ -158,13 +199,15 @@
     def _(i):
         remote(mine, picked.at[z], send.at[2], recv.at[2], line_peer(i)).start()
 
-    @pl.loop(1, SIDE_Z)
-    def _(i):
-        place = line_peer(i)
-        remote(stage.at[place[2]], whole.at[:, z], send.at[3], recv.at[3], place).start()
+    @pl.loop(EARLY, SIDE_Z - 1)
+    def _(k):
+        pass_on(k)
 
     picked[z] = mine[...]
     whole[:, z] = stage[z]
+    no_matter(
+        own.at[:, pl.ds(0, (PLANE - 1) * SIDE_Z * size)], send.at[1], recv.at[1]
+    ).wait_send()
     no_matter(picked.at[pl.ds(0, SIDE_Z - 1)], send.at[2], recv.at[2]).wait()
 
     values = jnp.swapaxes(picked[pl.ds(0, SIDE_Z)], 0, 1).reshape(members, watches)
@@ -247,47 +290,63 @@
 
     met(barrier)
 
-    @pl.loop(1, SIDE_Z)
-    def _(i):
-        place = line_peer(i)
-        remote(whole.at[:, place[2]], stage.at[z], send_z, recv_z.at[z], place).start()
-
-    def hand_on(source, block):
-        @pl.loop(1, PLANE)
+    @pl.loop(0, SIDE_Z - 1)
+    def _(k):
+        t = lax.rem(z + along(k), SIDE_Z)
+
+        @pl.loop(0, SIDE_Y)
+        def _(dy):
+            py = lax.rem(y + dy, SIDE_Y)
+            remote(
+                whole.at[py, t], stage.at[z, py], send_z, recv_z.at[z, py], (x, y, t, c)
+            ).start()
+
+    def hand_on(source, py, dy, block):
+        @pl.loop(jnp.where(dy == 0, 1, 0), CORES * SIDE_X)
         def _(j):
-            px, py, _, pc = plane_peer(j)
+            px = lax.rem(x + lax.rem(j, SIDE_X), SIDE_X)
+            pc = lax.rem(c + j // SIDE_X, CORES)
             remote(
-                source.at[py, pc * SIDE_X + px],
+                source.at[pc * SIDE_X + px],
                 own.at[:, links_of(block, size)],
                 send_p,
                 recv_p,
                 (px, py, z, pc),
             ).start()
 
-        own[:, links_of(block, size)] = source[y, c * SIDE_X + x]
-
-    hand_on(whole.at[:, z], block_of(x, y, z, c))
-
-    @pl.loop(1, SIDE_Z)
-    def _(i):
-        t = lax.rem(z + SIDE_Z - i, SIDE_Z)
-        remote(stage.at[t], stage.at[t], send_z, recv_z.at[t], (x, y, z, c)).wait_recv()
-        hand_on(stage.at[t], block_of(x, y, t, c))
-
-    arrived = stage.at[pl.ds(0, SIDE_Z - 1)]
-    remote(arrived, arrived, send_z, recv_z.at[0], (x, y, z, c)).wait_send()
-    arrived = own.at[:, pl.ds(0, (PLANE - 1) * SIDE_Z * size)]
-    remote(arrived, arrived, send_p, recv_p, (x, y, z, c)).wait()
+        @pl.when(dy == 0)
+        def _():
+            own[:, links_of(block, size)] = source[c * SIDE_X + x]
+
+    @pl.loop(0, SIDE_Y)
+    def _(dy):
+        py = lax.rem(y + dy, SIDE_Y)
+        hand_on(whole.at[py, z], py, dy, block_of(x, y, z, c))
+
+    @pl.loop(0, SIDE_Z - 1)
+    def _(k):
+        t = lax.rem(z + SIDE_Z - along(k), SIDE_Z)
+
+        @pl.loop(0, SIDE_Y)
+        def _(dy):
+            py = lax.rem(y + dy, SIDE_Y)
+            no_matter(stage.at[t, py], send_z, recv_z.at[t, py]).wait_recv()
+            hand_on(stage.at[t, py], py, dy, block_of(x, y, t, c))
+
+    no_matter(stage.at[pl.ds(0, SIDE_Z - 1)], send_z, recv_z.at[0, 0]).wait_send()
+    no_matter(own.at[:, pl.ds(0, (PLANE - 1) * SIDE_Z * size)], send_p, recv_p).wait()
 
 
 VMEM = pl.BlockSpec(memory_space=pltpu.VMEM)
 
 
-def gathered(own, notes, members):
+def gathered(own, offsets, observed, variances):
+    rows = own.shape[0]
     size = own.shape[1] // (PLANE * SIDE_Z)
+    members = rows * PLANE * SIDE_Z
     seats = CORES * SIDE_X
-    rows = own.shape[0]
-    watches = notes.shape[1]
+    count = offsets.shape[-1]
+    watches = SIDE_Z * count
     part = (members // CORES) // (SIDE_X * SIDE_Y)
     f32, bf16 = jnp.float32, jnp.bfloat16
     return pl.pallas_call(
@@ -298,12 +357,15 @@
             jax.ShapeDtypeStruct((members, members), f32),
             jax.ShapeDtypeStruct((2, members), f32),
         ),
-        in_specs=[VMEM, VMEM],
+        in_specs=[pl.BlockSpec(memory_space=pl.ANY)] * 4,
         out_specs=(VMEM, VMEM, VMEM),
         scratch_shapes=[
+            pltpu.VMEM(own.shape, bf16),
+            pltpu.VMEM((8, count), f32),
+            pltpu.VMEM((1, count), jnp.int32),
             pltpu.VMEM((SIDE_Z, SIDE_Y, seats, rows, size), bf16),
             pltpu.VMEM((SIDE_Z, SIDE_Y, seats * rows, size), bf16),
-            pltpu.VMEM((SIDE_Z, *notes.shape), f32),
+            pltpu.VMEM((SIDE_Z + 1, 8, watches), f32),
             pltpu.VMEM((size, watches), bf16),
             pltpu.VMEM((SIDE_Z + 1, SIDE_Y, seats * rows, watches), bf16),
             pltpu.VMEM((members, members), f32),
@@ -311,11 +373,13 @@
             pltpu.VMEM((SIDE_X * SIDE_Y, part, members), f32),
             pltpu.VMEM((PLANE + 1, 2, members), f32),
             pltpu.VMEM((members // CORES, members), f32),
+            pltpu.SemaphoreType.DMA((4,)),
             pltpu.SemaphoreType.DMA((9,)),
             pltpu.SemaphoreType.DMA((9,)),
+            pltpu.SemaphoreType.DMA((SIDE_Z,)),
         ],
         compiler_params=pltpu.CompilerParams(collective_id=0, has_side_effects=True),
-    )(own, notes)
+    )(own, offsets, observed, variances)
 
 
 def scattered(high, low, state, own_rows):
@@ -331,7 +395,7 @@
             pltpu.VMEM(shape, state.dtype),
             pltpu.VMEM((SIDE_Z, SIDE_Y, *shape[2:]), state.dtype),
             pltpu.SemaphoreType.DMA,
-            pltpu.SemaphoreType.DMA((SIDE_Z,)),
+            pltpu.SemaphoreType.DMA((SIDE_Z, SIDE_Y)),
             pltpu.SemaphoreType.DMA,
             pltpu.SemaphoreType.DMA,
         ],
@@ -350,18 +414,12 @@
     )
 
 
-def dot3(a, b):
-    ah, al = split_bf16(a)
-    bh, bl = split_bf16(b)
-    return dot1(ah, bh) + (dot1(ah, bl) + dot1(al, bh))
-
-
 def dot6(a, b):
     return jnp.dot(a, b, precision=lax.Precision.HIGHEST, preferred_element_type=jnp.float32)
 
 
 TILE = 128
-WELL_CONDITIONED = 600.0
+WELL_CONDITIONED = 2000.0
 ROUNDING = 1e-6
 
 
@@ -380,121 +438,191 @@
     return jnp.sum(m * m)
 
 
-def unit(rows, n):
-    row = lax.broadcasted_iota(jnp.int32, (TILE, n), 0) + rows.start
+def unit(rows, n, first=0):
+    row = lax.broadcasted_iota(jnp.int32, (TILE, n), 0) + (rows.start - first)
     col = lax.broadcasted_iota(jnp.int32, (TILE, n), 1)
     return jnp.where(row == col, 1.0, 0.0).astype(jnp.float32)
 
 
-def inverse_into(x, system, r, tmp):
-    n = system.shape[0]
-
-    def series(dot, enough):
-        def square(rows, bound):
-            tmp[rows, :] = dot(system[rows, :], system[...])
-            return jnp.maximum(bound, largest_row(tmp[rows, :]))
-
-        bound = jnp.sqrt(by_rows(n, square, jnp.float32(0.0)) * 1.02)
-        a = 2.0 / (1.0 + bound)
-
-        def first(rows, total):
-            eye = unit(rows, n)
-            s = system[rows, :] * a
-            x[rows, :] = a * (2.0 * eye - s)
-            left = eye - 2.0 * s + (a * a) * tmp[rows, :]
+EXTRA = 16
+
+
+def residual_squares(left):
+    return jnp.sum(jnp.sum(left * left, axis=0, keepdims=True))
+
+
+def quick_inverse(x, system, r, parts, both):
+    n = system.shape[1]
+    rows = system.shape[0]
+
+    def passes(lhs, rhs):
+        return jnp.dot(lhs, rhs, preferred_element_type=jnp.float32)
+
+    values = system[...]
+    high = values.astype(jnp.bfloat16)
+    parts[pl.ds(0, rows), :] = high
+    parts[pl.ds(rows, rows), :] = (values - high.astype(jnp.float32)).astype(jnp.bfloat16)
+    top = pl.ds(0, n)
+    r[...] = passes(parts[top, :], parts[top, :])
+    bound = jnp.sqrt(jnp.max(jnp.sum(jnp.abs(r[...]), axis=0, keepdims=True)) * 1.02)
+    a = 2.0 / (1.0 + bound)
+
+    def first(rows, total):
+        eye = unit(rows, n)
+        s = system[rows, :] * a
+        left = eye - 2.0 * s + (a * a) * r[rows, :]
+        grown = a * (2.0 * eye - s)
+        x[rows, :] = grown
+        both[rows, :] = grown.astype(jnp.bfloat16)
+        both[pl.ds(n + rows.start, TILE), :] = left.astype(jnp.bfloat16)
+        return total + jnp.sum(left * left, axis=0, keepdims=True)
+
+    total = by_rows(n, first, jnp.zeros((1, n), jnp.float32))
+
+    def more(state):
+        count, size = state
+        return jnp.logical_and(count < 16, size > 0.01)
+
+    def double(state):
+        count, _ = state
+        out = passes(both[...], both[pl.ds(n, n), :])
+        grown = x[top, :] + out[:n]
+        left = out[n:]
+        x[top, :] = grown
+        both[...] = jnp.concatenate([grown, left]).astype(jnp.bfloat16)
+        return count + 1, residual_squares(left)
+
+    lax.while_loop(more, double, (jnp.int32(0), jnp.sum(total)))
+
+    def more_newton(state):
+        count, size = state
+        return jnp.logical_and(count < 8, size > ROUNDING)
+
+    def newton(state):
+        count, _ = state
+        now = x[top, :]
+        xh = now.astype(jnp.bfloat16)
+        xl = (now - xh.astype(jnp.float32)).astype(jnp.bfloat16)
+        here_high = parts[pl.ds(0, rows), :]
+        out = passes(here_high, xh) + (
+            passes(here_high, xl) + passes(parts[pl.ds(rows, rows), :], xh)
+        )
+        r[...] = out[:n]
+
+        def left_of(at, total):
+            left = unit(at, n) - r[at, :]
+            both[at, :] = left.astype(jnp.bfloat16)
+            return total + jnp.sum(left * left, axis=0, keepdims=True)
+
+        total = by_rows(n, left_of, jnp.zeros((1, n), jnp.float32))
+        tail = out[n:]
+        grown = jnp.concatenate([now, tail])
+        x[...] = grown + passes(jnp.concatenate([xh, tail.astype(jnp.bfloat16)]), both[top, :])
+        return count + 1, jnp.sum(total)
+
+    return lax.while_loop(more_newton, newton, (jnp.int32(0), jnp.float32(1.0)))[1]
+
+
+def careful_inverse(x, system, r, tmp):
+    n = system.shape[1]
+
+    def square(rows, bound):
+        tmp[rows, :] = dot6(system[rows, :], system[pl.ds(0, n), :])
+        return jnp.maximum(bound, largest_row(tmp[rows, :]))
+
+    bound = jnp.sqrt(by_rows(n, square, jnp.float32(0.0)) * 1.02)
+    a = 2.0 / (1.0 + bound)
+
+    def first(rows, total):
+        eye = unit(rows, n)
+        s = system[rows, :] * a
+        x[rows, :] = a * (2.0 * eye - s)
+        left = eye - 2.0 * s + (a * a) * tmp[rows, :]
+        r[rows, :] = left
+        return total + sum_of_squares(left)
+
+    def more(state):
+        count, size = state
+        return jnp.logical_and(count < 40, size > 4e-4)
+
+    def double(state):
+        def grow(rows, _):
+            x[rows, :] += dot6(x[rows, :], r[...])
+            tmp[rows, :] = dot6(r[rows, :], r[...])
+            return 0
+
+        by_rows(n, grow, 0)
+
+        def take(rows, total):
+            left = tmp[rows, :]
             r[rows, :] = left
             return total + sum_of_squares(left)
 
-        size = by_rows(n, first, jnp.float32(0.0))
-
-        def more(state):
-            count, size = state
-            return jnp.logical_and(count < 40, size > enough * enough)
-
-        def double(state):
-            count, _ = state
-
-            def grow(rows, _):
-                x[rows, :] += dot(x[rows, :], r[...])
-                tmp[rows, :] = dot(r[rows, :], r[...])
-                return 0
-
-            by_rows(n, grow, 0)
-
-            def take(rows, total):
-                left = tmp[rows, :]
-                r[rows, :] = left
-                return total + sum_of_squares(left)
-
-            return count + 1, by_rows(n, take, jnp.float32(0.0))
-
-        lax.while_loop(more, double, (jnp.int32(0), size))
-
-    def newton(dot, dot_step):
-        def more(state):
-            count, size = state
-            return jnp.logical_and(count < 12, size > ROUNDING)
-
-        def step(state):
-            count, _ = state
-
-            def residual(rows, total):
-                left = unit(rows, n) - dot(system[rows, :], x[...])
-                r[rows, :] = left
-                return total + sum_of_squares(left)
-
-            size = by_rows(n, residual, jnp.float32(0.0))
-
-            def correct(rows, _):
-                x[rows, :] += dot_step(x[rows, :], r[...])
-                return 0
-
-            by_rows(n, correct, 0)
-            return count + 1, size
-
-        return lax.while_loop(more, step, (jnp.int32(0), jnp.float32(1.0)))[1]
-
-    bound = by_rows(n, lambda rows, m: jnp.maximum(m, largest_row(system[rows, :])), jnp.float32(0.0))
-    easy = bound < WELL_CONDITIONED
-
-    def quick():
-        series(dot1, 0.1)
-        return newton(dot3, dot3)
-
-    left = lax.cond(easy, quick, lambda: jnp.float32(1.0))
-
-    @pl.when(jnp.logical_not(left <= ROUNDING))
-    def _():
-        series(dot6, 0.02)
-        newton(dot6, dot6)
-
-
-def mixing_kernel(products, sums, high, low, x, system, r, tmp):
+        return state[0] + 1, by_rows(n, take, jnp.float32(0.0))
+
+    lax.while_loop(more, double, (jnp.int32(0), by_rows(n, first, jnp.float32(0.0))))
+
+    def more_newton(state):
+        count, size = state
+        return jnp.logical_and(count < 12, size > ROUNDING)
+
+    def newton(state):
+        def residual(rows, total):
+            left = unit(rows, n) - dot6(system[rows, :], x[pl.ds(0, n), :])
+            r[rows, :] = left
+            return total + sum_of_squares(left)
+
+        size = by_rows(n, residual, jnp.float32(0.0))
+
+        def correct(rows, _):
+            x[rows, :] += dot6(x[rows, :], r[...])
+            return 0
+
+        by_rows(n, correct, 0)
+        return state[0] + 1, size
+
+    lax.while_loop(more_newton, newton, (jnp.int32(0), jnp.float32(1.0)))
+    last = pl.ds(n, system.shape[0] - n)
+    x[last, :] = dot6(system[last, :], x[pl.ds(0, n), :])
+
+
+def mixing_kernel(products, sums, high, low, x, system, r, parts, both):
     n = products.shape[0]
     square = jnp.sum(sums[1:2, 0:1] / sums[1:2, 1:2])
     inflation = jnp.sqrt(jnp.full((1, n), square, jnp.float32))
 
-    def scaled(rows, trace):
-        eye = unit(rows, n)
-        p = products[rows, :] * square
-        system[rows, :] = eye + p
-        return trace + jnp.sum(eye * p)
-
-    trace = by_rows(n, scaled, jnp.float32(0.0))
+    def traced(rows, trace):
+        eye = unit(rows, TILE, rows.start)
+        return trace + jnp.sum(eye * products[rows, rows], axis=0, keepdims=True)
+
+    trace = jnp.sum(by_rows(n, traced, jnp.zeros((1, TILE), jnp.float32))) * square
     shift = trace / ((n - 1.0) * n)
 
-    def shifted(rows, _):
-        system[rows, :] += shift
-        return 0
-
-    by_rows(n, shifted, 0)
-    inverse_into(x, system, r, tmp)
-
-    q = dot6(sums[0:1, :], x[...])
+    def scaled(rows, most):
+        s = unit(rows, n) + (products[rows, :] * square + shift)
+        system[rows, :] = s
+        return most + jnp.sum(jnp.abs(s), axis=0, keepdims=True)
+
+    most = jnp.max(by_rows(n, scaled, jnp.zeros((1, n), jnp.float32)))
+    first = lax.broadcasted_iota(jnp.int32, (EXTRA, n), 0) == 0
+    system[pl.ds(n, EXTRA), :] = jnp.where(first, sums[0:1, :], 0.0)
+    left = lax.cond(
+        most < WELL_CONDITIONED,
+        lambda: quick_inverse(x, system, r, parts, both),
+        lambda: jnp.float32(1.0),
+    )
+
+    @pl.when(jnp.logical_not(left <= ROUNDING))
+    def _():
+        pl.run_scoped(
+            lambda tmp: careful_inverse(x, system, r, tmp), pltpu.VMEM((n, n), jnp.float32)
+        )
+
+    q = x[pl.ds(n, 1), :] * square
 
     def mix(rows, _):
         eye = unit(rows, n)
-        mixing = 0.5 * inflation * (eye + x[rows, :]) + square * q
+        mixing = (0.5 * inflation) * (eye + x[rows, :]) + q
         mean = jnp.sum(mixing, axis=1, keepdims=True) * (1.0 / n)
         high[rows, :], low[rows, :] = split_bf16(mixing - mean + 1.0 / n)
         return 0
@@ -510,23 +638,37 @@
         out_shape=[jax.ShapeDtypeStruct((n, n), jnp.bfloat16)] * 2,
         in_specs=[VMEM, VMEM],
         out_specs=[VMEM, VMEM],
-        scratch_shapes=[pltpu.VMEM((n, n), jnp.float32) for _ in range(4)],
+        scratch_shapes=[
+            pltpu.VMEM((n + EXTRA, n), jnp.float32),
+            pltpu.VMEM((n + EXTRA, n), jnp.float32),
+            pltpu.VMEM((n, n), jnp.float32),
+            pltpu.VMEM((2 * (n + EXTRA), n), jnp.bfloat16),
+            pltpu.VMEM((2 * n, n), jnp.bfloat16),
+        ],
     )(products, sums)
 
 
+def put_out_kernel(own, out, done):
+    copy = pltpu.make_async_copy(own, out, done)
+    copy.start()
+    copy.wait()
+
+
+def put_out(own):
+    return pl.pallas_call(
+        put_out_kernel,
+        name="put_out",
+        out_shape=jax.ShapeDtypeStruct(own.shape, own.dtype),
+        in_specs=[VMEM],
+        out_specs=pl.BlockSpec(memory_space=pl.ANY),
+        scratch_shapes=[pltpu.SemaphoreType.DMA],
+    )(own)
+
+
 def local(ensemble, obs_offset, observed, obs_var):
-    own_rows = ensemble.shape[0]
-    members = own_rows * PLANE * SIDE_Z
-    count = obs_offset.size
-    notes = jnp.concatenate(
-        [obs_offset.astype(jnp.float32).reshape(1, -1), observed.reshape(1, -1), obs_var.reshape(1, -1)]
-    )
-    notes = jnp.pad(notes, ((0, 5), (0, 0)))
-    seat = lax.broadcasted_iota(jnp.int32, (8, SIDE_Z * count), 1) // count
-    notes = jnp.where(seat == lax.axis_index("member_1"), jnp.tile(notes, (1, SIDE_Z)), 0.0)
-    state, products, sums = gathered(ensemble, notes, members)
+    state, products, sums = gathered(ensemble, obs_offset, observed, obs_var)
     high, low = mixed(products, sums)
-    return scattered(high, low, state.reshape(members, -1), own_rows)
+    return put_out(scattered(high, low, state.reshape(len(products), -1), len(ensemble)))
 
 
 def solution(mesh):

time: 210 us -> 196 us (0.933)
  Pallas kernels: 205 us -> 196 us
  local copies, waits for them, and re-layouts: 3.97 us -> 0 us
    pallas_call x1, Pallas kernels: 48.2 us -> 39.8 us  [scattered(): pl.pallas_call(scatter_kernel, name='scatter', out_shape=jax.ShapeDtypeSt...]
    unnamed x7 -> x0, local copies, waits for them, and re-layouts: 3.89 us -> none
    pallas_call x0 -> x1, Pallas kernels: none -> 2.2 us  [put_out(): pl.pallas_call(put_out_kernel, name='put_out', out_shape=jax.ShapeDtypeSt...]
where the time goes in v3:
time: 196 us
  Pallas kernels  196 us (100%)
    pallas_call x1, Pallas kernels, mixed(): pl.pallas_call(mixing_kernel, name='mixing', out_shape=[jax.ShapeDtypeStr...  94.8 us
    pallas_call x1, Pallas kernels, gathered(): pl.pallas_call(gather_kernel, name='gather', out_shape=(jax.ShapeDtypeStr...  59.4 us
    pallas_call x1, Pallas kernels, scattered(): pl.pallas_call(scatter_kernel, name='scatter', out_shape=jax.ShapeDtypeSt...  39.8 us

profile of v3, /device:TPU:1, one launch (start us, length us, event | category | flops | bytes accessed | tf_op | source)
XLA Modules:
  0.0 196.3 jit_solution(4509810484813690721)
XLA Ops:
  0.0 59.4 %gather.1 = (bf16[4,8,16,1024]{3,2,1,0:T(8,128)(2,1)}, f32[512,512]{1,0:T(8,128)}, f32[2,512]{1,0:T(2,128)}) custom-call(bf16[2,262144]{1,0:T(2,128)(2,1)} %ensemble.1, s32[1,1,16]{2,1,0:T(1,128)} %offsets.1, f32[1,1,16]{2,1,0:T(1,128)} %observed.1, f32[1,1,16]{2,1,0:T(1,128)} %variances.1), custom_call_target="tpu_custom_call" | custom-call | tf_op jit(solution)/shard_map/gather/pallas_call | solution.py:352
  59.4 94.8 %mixing.1 = (bf16[512,512]{1,0:T(8,128)(2,1)}, bf16[512,512]{1,0:T(8,128)(2,1)}) custom-call(f32[512,512]{1,0:T(8,128)} %get-tuple-element.10.products, f32[2,512]{1,0:T(2,128)} %get-tuple-element.11.sums), custom_call_target="tpu_custom_call" | custom-call | tf_op jit(solution)/shard_map/mixing/pallas_call | solution.py:635
  154.2 39.8 %scatter.1.own = bf16[2,262144]{1,0:T(2,128)(2,1)} custom-call(bf16[512,512]{1,0:T(8,128)(2,1)} %get-tuple-element.12.high, bf16[512,512]{1,0:T(8,128)(2,1)} %get-tuple-element.13.low, bf16[512,1024]{1,0:T(8,128)(2,1)} %bitcast.1), custom_call_target="tpu_custom_call" | custom-call | tf_op jit(solution)/shard_map/scatter/pallas_call | solution.py:388
  194.1 2.2 %put_out.1 = bf16[2,262144]{1,0:T(2,128)(2,1)} custom-call(bf16[2,262144]{1,0:T(2,128)(2,1)} %scatter.1.own), custom_call_target="tpu_custom_call" | custom-call | tf_op jit(solution)/shard_map/put_out/pallas_call | solution.py:658

commit v4 on v3

--- a/solution.py
+++ b/solution.py
@@ -12,6 +12,7 @@
 
 MESH_ID = pl.DeviceIdType.MESH
 SIDE_Y, SIDE_Z, CORES, SIDE_X = 4, 8, 2, 4
+TILE = 128
 
 
 def here():
@@ -97,7 +98,7 @@
     return lax.rem(jnp.where(lax.rem(k, 2) == 0, d, SIDE_Z - d), SIDE_Z) * jnp.where(k == 7, 0, 1)
 
 
-EARLY = 4
+EARLY = 2
 
 
 def gather_kernel(
@@ -107,7 +108,7 @@
 ):
     x, y, z, c = here()
     size = own.shape[1] // (PLANE * SIDE_Z)
-    members = total.shape[0]
+    members = sums.shape[1]
     seat = c * SIDE_X + x
     loads = [
         pltpu.make_async_copy(ensemble, own, copied.at[0]),
@@ -224,13 +225,18 @@
     extra = extras.at[PLANE]
     extra[0:1, :] = column
     extra[1:2, :] = jnp.where(lane == 0, numer, jnp.where(lane == 1, denom, 0.0))
-    product[...] = dot6_t(anomaly * weight, anomaly)
-
-    rows = members // CORES
-    kept = pl.ds(pl.multiple_of(c * rows, rows), rows)
-    given = pl.ds(pl.multiple_of((1 - c) * rows, rows), rows)
+    weighted = anomaly * weight
+    block = 0
+    for i in range(members // TILE):
+        row = dot6_t(weighted[i * TILE : (i + 1) * TILE], anomaly[: (i + 1) * TILE])
+        for j in range(i + 1):
+            core, at = divmod(block, product.shape[1] // TILE)
+            product[core, at * TILE : (at + 1) * TILE, :] = row[:, j * TILE : (j + 1) * TILE]
+            block += 1
+
+    rows = product.shape[1]
     partner = (x, y, z, 1 - c)
-    remote(product.at[given], other, send.at[4], recv.at[4], partner).start()
+    remote(product.at[1 - c], other, send.at[4], recv.at[4], partner).start()
 
     @pl.loop(1, PLANE)
     def _(i):
@@ -240,12 +246,12 @@
 
     extras[y * (CORES * SIDE_X) + seat] = extra[...]
     no_matter(other, send.at[4], recv.at[4]).wait()
-    half[...] = product[kept, :] + other[...]
+    half[...] = product[c] + other[...]
     chips = SIDE_X * SIDE_Y
     part = rows // chips
 
-    def part_of(px, py, base=0):
-        return pl.ds(pl.multiple_of(base + (py * SIDE_X + px) * part, part), part)
+    def part_of(px, py):
+        return pl.ds(pl.multiple_of((py * SIDE_X + px) * part, part), part)
 
     @pl.loop(1, chips)
     def _(i):
@@ -260,7 +266,7 @@
 
     chunks[y * SIDE_X + x] = half[part_of(x, y), :]
     no_matter(chunks.at[pl.ds(0, chips - 1)], send.at[6], recv.at[6]).wait()
-    done = total.at[part_of(x, y, c * rows)]
+    done = total.at[c, part_of(x, y)]
     done[...] = jnp.sum(chunks[...], axis=0)
 
     @pl.loop(1, chips)
@@ -268,7 +274,7 @@
         remote(done, done, send.at[7], recv.at[7], chip_peer(i)).start()
 
     no_matter(half.at[pl.ds(0, rows - part)], send.at[7], recv.at[7]).wait()
-    remote(total.at[kept], total.at[kept], send.at[8], recv.at[8], partner).start()
+    remote(total.at[c], total.at[c], send.at[8], recv.at[8], partner).start()
     no_matter(extras.at[pl.ds(0, PLANE - 1)], send.at[5], recv.at[5]).wait()
     sums[...] = jnp.sum(extras[pl.ds(0, PLANE)], axis=0)
     no_matter(other, send.at[8], recv.at[8]).wait()
@@ -338,6 +344,7 @@
 
 
 VMEM = pl.BlockSpec(memory_space=pltpu.VMEM)
+ROOM = 24 << 20
 
 
 def gathered(own, offsets, observed, variances):
@@ -347,17 +354,19 @@
     seats = CORES * SIDE_X
     count = offsets.shape[-1]
     watches = SIDE_Z * count
-    part = (members // CORES) // (SIDE_X * SIDE_Y)
+    tiles = members // TILE
+    packed = tiles * (tiles + 1) // 2 * TILE // CORES
+    part = packed // (SIDE_X * SIDE_Y)
     f32, bf16 = jnp.float32, jnp.bfloat16
     return pl.pallas_call(
         gather_kernel,
         name="gather",
         out_shape=(
             jax.ShapeDtypeStruct((SIDE_Y, SIDE_Z, seats * rows, size), bf16),
-            jax.ShapeDtypeStruct((members, members), f32),
+            jax.ShapeDtypeStruct((CORES, packed, TILE), f32),
             jax.ShapeDtypeStruct((2, members), f32),
         ),
-        in_specs=[pl.BlockSpec(memory_space=pl.ANY)] * 4,
+        in_specs=[pl.BlockSpec(memory_space=pltpu.HBM)] * 4,
         out_specs=(VMEM, VMEM, VMEM),
         scratch_shapes=[
             pltpu.VMEM(own.shape, bf16),
@@ -368,18 +377,20 @@
             pltpu.VMEM((SIDE_Z + 1, 8, watches), f32),
             pltpu.VMEM((size, watches), bf16),
             pltpu.VMEM((SIDE_Z + 1, SIDE_Y, seats * rows, watches), bf16),
-            pltpu.VMEM((members, members), f32),
-            pltpu.VMEM((members // CORES, members), f32),
-            pltpu.VMEM((SIDE_X * SIDE_Y, part, members), f32),
+            pltpu.VMEM((CORES, packed, TILE), f32),
+            pltpu.VMEM((packed, TILE), f32),
+            pltpu.VMEM((SIDE_X * SIDE_Y, part, TILE), f32),
             pltpu.VMEM((PLANE + 1, 2, members), f32),
-            pltpu.VMEM((members // CORES, members), f32),
+            pltpu.VMEM((packed, TILE), f32),
             pltpu.SemaphoreType.DMA((4,)),
             pltpu.SemaphoreType.DMA((9,)),
             pltpu.SemaphoreType.DMA((9,)),
             pltpu.SemaphoreType.DMA((SIDE_Z,)),
         ],
-        compiler_params=pltpu.CompilerParams(collective_id=0, has_side_effects=True),
-    )(own, offsets, observed, variances)
+        compiler_params=pltpu.CompilerParams(
+            collective_id=0, has_side_effects=True, vmem_limit_bytes=ROOM
+        ),
+    )(*(pltpu.with_memory_space_constraint(a, pltpu.HBM) for a in (own, offsets, observed, variances)))
 
 
 def scattered(high, low, state, own_rows):
@@ -399,7 +410,9 @@
             pltpu.SemaphoreType.DMA,
             pltpu.SemaphoreType.DMA,
         ],
-        compiler_params=pltpu.CompilerParams(collective_id=1, has_side_effects=True),
+        compiler_params=pltpu.CompilerParams(
+            collective_id=1, has_side_effects=True, vmem_limit_bytes=ROOM
+        ),
     )(high, low, state)
 
 
@@ -418,7 +431,6 @@
     return jnp.dot(a, b, precision=lax.Precision.HIGHEST, preferred_element_type=jnp.float32)
 
 
-TILE = 128
 WELL_CONDITIONED = 2000.0
 ROUNDING = 1e-6
 
@@ -438,8 +450,8 @@
     return jnp.sum(m * m)
 
 
-def unit(rows, n, first=0):
-    row = lax.broadcasted_iota(jnp.int32, (TILE, n), 0) + (rows.start - first)
+def unit(rows, n):
+    row = lax.broadcasted_iota(jnp.int32, (TILE, n), 0) + rows.start
     col = lax.broadcasted_iota(jnp.int32, (TILE, n), 1)
     return jnp.where(row == col, 1.0, 0.0).astype(jnp.float32)
 
@@ -587,23 +599,34 @@
 
 
 def mixing_kernel(products, sums, high, low, x, system, r, parts, both):
-    n = products.shape[0]
+    n = sums.shape[1]
+    tiles = n // TILE
     square = jnp.sum(sums[1:2, 0:1] / sums[1:2, 1:2])
     inflation = jnp.sqrt(jnp.full((1, n), square, jnp.float32))
-
-    def traced(rows, trace):
-        eye = unit(rows, TILE, rows.start)
-        return trace + jnp.sum(eye * products[rows, rows], axis=0, keepdims=True)
-
-    trace = jnp.sum(by_rows(n, traced, jnp.zeros((1, TILE), jnp.float32))) * square
+    row = lax.broadcasted_iota(jnp.int32, (TILE, TILE), 0)
+    col = lax.broadcasted_iota(jnp.int32, (TILE, TILE), 1)
+    eye = jnp.where(row == col, 1.0, 0.0).astype(jnp.float32)
+    corners = [i * (i + 3) // 2 for i in range(tiles)]
+    diagonal = sum(products[block] for block in corners)
+    trace = jnp.sum(jnp.sum(eye * diagonal, axis=0, keepdims=True)) * square
     shift = trace / ((n - 1.0) * n)
-
-    def scaled(rows, most):
-        s = unit(rows, n) + (products[rows, :] * square + shift)
-        system[rows, :] = s
-        return most + jnp.sum(jnp.abs(s), axis=0, keepdims=True)
-
-    most = jnp.max(by_rows(n, scaled, jnp.zeros((1, n), jnp.float32)))
+    block = 0
+    for i in range(tiles):
+        down = pl.ds(i * TILE, TILE)
+        for j in range(i + 1):
+            across = pl.ds(j * TILE, TILE)
+            values = products[block] * square + shift
+            if i == j:
+                system[down, down] = values + eye
+            else:
+                system[down, across] = values
+                system[across, down] = values.T
+            block += 1
+
+    def longest(rows, most):
+        return most + jnp.sum(jnp.abs(system[rows, :]), axis=0, keepdims=True)
+
+    most = jnp.max(by_rows(n, longest, jnp.zeros((1, n), jnp.float32)))
     first = lax.broadcasted_iota(jnp.int32, (EXTRA, n), 0) == 0
     system[pl.ds(n, EXTRA), :] = jnp.where(first, sums[0:1, :], 0.0)
     left = lax.cond(
@@ -631,7 +654,7 @@
 
 
 def mixed(products, sums):
-    n = products.shape[0]
+    n = sums.shape[1]
     return pl.pallas_call(
         mixing_kernel,
         name="mixing",
@@ -645,7 +668,8 @@
             pltpu.VMEM((2 * (n + EXTRA), n), jnp.bfloat16),
             pltpu.VMEM((2 * n, n), jnp.bfloat16),
         ],
-    )(products, sums)
+        compiler_params=pltpu.CompilerParams(vmem_limit_bytes=ROOM),
+    )(products.reshape(-1, TILE, TILE), sums)
 
 
 def put_out_kernel(own, out, done):
@@ -660,15 +684,16 @@
         name="put_out",
         out_shape=jax.ShapeDtypeStruct(own.shape, own.dtype),
         in_specs=[VMEM],
-        out_specs=pl.BlockSpec(memory_space=pl.ANY),
+        out_specs=pl.BlockSpec(memory_space=pltpu.HBM),
         scratch_shapes=[pltpu.SemaphoreType.DMA],
+        compiler_params=pltpu.CompilerParams(vmem_limit_bytes=ROOM),
     )(own)
 
 
 def local(ensemble, obs_offset, observed, obs_var):
     state, products, sums = gathered(ensemble, obs_offset, observed, obs_var)
     high, low = mixed(products, sums)
-    return put_out(scattered(high, low, state.reshape(len(products), -1), len(ensemble)))
+    return put_out(scattered(high, low, state.reshape(sums.shape[1], -1), len(ensemble)))
 
 
 def solution(mesh):

time: 196 us -> 181 us (0.923)
  Pallas kernels: 196 us -> 181 us
    pallas_call x1, Pallas kernels: 59.4 us -> 51.9 us  [gathered(): pl.pallas_call(gather_kernel, name='gather', out_shape=(jax.ShapeDtypeStr...]
    pallas_call x1, Pallas kernels: 39.8 us -> 35.8 us  [scattered(): pl.pallas_call(scatter_kernel, name='scatter', out_shape=jax.ShapeDtypeSt...]
    pallas_call x1, Pallas kernels: 94.8 us -> 92.6 us  [mixed(): pl.pallas_call(mixing_kernel, name='mixing', out_shape=[jax.ShapeDtypeStr...]
where the time goes in v4:
time: 181 us
  Pallas kernels  181 us (100%)
    pallas_call x1, Pallas kernels, mixed(): pl.pallas_call(mixing_kernel, name='mixing', out_shape=[jax.ShapeDtypeStr...  92.6 us
    pallas_call x1, Pallas kernels, gathered(): pl.pallas_call(gather_kernel, name='gather', out_shape=(jax.ShapeDtypeStr...  51.9 us
    pallas_call x1, Pallas kernels, scattered(): pl.pallas_call(scatter_kernel, name='scatter', out_shape=jax.ShapeDtypeSt...  35.8 us

profile of v4, /device:TPU:1, one launch (start us, length us, event | category | flops | bytes accessed | tf_op | source)
XLA Modules:
  0.0 181.3 jit_solution(3183851004984887157)
XLA Ops:
  0.0 51.9 %gather.1 = (bf16[4,8,16,1024]{3,2,1,0:T(8,128)(2,1)S(1)}, f32[2,640,128]{2,1,0:T(8,128)S(1)}, f32[2,512]{1,0:T(2,128)S(1)}) custom-call(bf16[2,262144]{1,0:T(2,128)(2,1)} %ensemble.1, s32[1,1,16]{2,1,0:T(1,128)} %offsets.1, f32[1,1,16]{2,1,0:T(1,128)} %observed.1, f32[1,1,16]{2,1,0:T(1,128)} %variances.1), custom_call_target="tpu_custom_call" | custom-call | tf_op jit(solution)/shard_map/gather/pallas_call | solution.py:361
  51.9 92.6 %mixing.1 = (bf16[512,512]{1,0:T(8,128)(2,1)S(1)}, bf16[512,512]{1,0:T(8,128)(2,1)S(1)}) custom-call(f32[10,128,128]{2,1,0:T(8,128)S(1)} %bitcast.3, f32[2,512]{1,0:T(2,128)S(1)} %get-tuple-element.11.sums), custom_call_target="tpu_custom_call" | custom-call | tf_op jit(solution)/shard_map/mixing/pallas_call | solution.py:658
  144.5 35.8 %scatter.1.own = bf16[2,262144]{1,0:T(2,128)(2,1)S(1)} custom-call(bf16[512,512]{1,0:T(8,128)(2,1)S(1)} %get-tuple-element.12.high, bf16[512,512]{1,0:T(8,128)(2,1)S(1)} %get-tuple-element.13.low, bf16[512,1024]{1,0:T(8,128)(2,1)S(1)} %bitcast.2), custom_call_target="tpu_custom_call" | custom-call | tf_op jit(solution)/shard_map/scatter/pallas_call | solution.py:399
  180.3 1.0 put_out.1

commit v5 on v4

--- a/solution.py
+++ b/solution.py
@@ -30,6 +30,7 @@
 
 def chip_peer(i):
     x, y, z, c = here()
+    i = lax.rem(i * 7, SIDE_X * SIDE_Y)
     return lax.rem(x + i, SIDE_X), lax.rem(y + i // SIDE_X, SIDE_Y), z, c
 
 
@@ -42,7 +43,7 @@
 
 def plane_peer(i):
     x, y, z, c = here()
-    dy, dc, dx = in_plane(i)
+    dy, dc, dx = in_plane(lax.rem(i * 13, PLANE))
     return lax.rem(x + dx, SIDE_X), lax.rem(y + dy, SIDE_Y), z, lax.rem(c + dc, CORES)
 
 
@@ -99,12 +100,13 @@
 
 
 EARLY = 2
+HALFWAY = 4
 
 
 def gather_kernel(
     ensemble, offsets, observed, variances, whole, total, sums,
     own, notes, numbers, pieces, stage, all_notes, seen, picked, product, half, chunks, extras,
-    other, copied, send, recv, arrived,
+    other, copied, send, recv, arrived, parted,
 ):
     x, y, z, c = here()
     size = own.shape[1] // (PLANE * SIDE_Z)
@@ -271,19 +273,34 @@
 
     @pl.loop(1, chips)
     def _(i):
-        remote(done, done, send.at[7], recv.at[7], chip_peer(i)).start()
-
-    no_matter(half.at[pl.ds(0, rows - part)], send.at[7], recv.at[7]).wait()
-    remote(total.at[c], total.at[c], send.at[8], recv.at[8], partner).start()
+        place = chip_peer(i)
+        remote(done, done, send.at[7], parted.at[y * SIDE_X + x], place).start()
+
+    remote(done, done, send.at[8], recv.at[8], partner).start()
+
+    @pl.loop(1, chips)
+    def _(i):
+        px, py, _, _ = chip_peer(chips - i)
+        piece = total.at[c, part_of(px, py)]
+        no_matter(piece, send.at[7], parted.at[py * SIDE_X + px]).wait_recv()
+        remote(piece, piece, send.at[8], recv.at[8], partner).start()
+
+    no_matter(half.at[pl.ds(0, rows - part)], send.at[7], recv.at[7]).wait_send()
     no_matter(extras.at[pl.ds(0, PLANE - 1)], send.at[5], recv.at[5]).wait()
     sums[...] = jnp.sum(extras[pl.ds(0, PLANE)], axis=0)
     no_matter(other, send.at[8], recv.at[8]).wait()
     no_matter(stage.at[pl.ds(0, SIDE_Z - 1)], send.at[3], recv.at[3]).wait()
 
 
-def scatter_kernel(high, low, state, own, whole, stage, send_z, recv_z, send_p, recv_p):
+def scatter_kernel(
+    high, low, state, own, whole, far, near, send_far, arrived, send_near, recv_near,
+    send_last, recv_last, send_own, recv_own,
+):
     x, y, z, c = here()
     rows, size = state.shape
+    chip, seat = x * SIDE_Y + y, c * SIDE_X + x
+    cut = far.shape[-1]
+    first, second = pl.ds(0, cut), pl.ds(cut, size - cut)
     barrier = pltpu.get_barrier_semaphore()
     greet(barrier)
     wide = 256
@@ -304,43 +321,79 @@
         def _(dy):
             py = lax.rem(y + dy, SIDE_Y)
             remote(
-                whole.at[py, t], stage.at[z, py], send_z, recv_z.at[z, py], (x, y, t, c)
+                whole.at[py, t, :, :, first],
+                far.at[z * SIDE_Y + py],
+                send_far,
+                arrived.at[z, py],
+                (x, y, t, c),
             ).start()
 
-    def hand_on(source, py, dy, block):
+    @pl.loop(1, PLANE)
+    def _(i):
+        px, py, _, pc = plane_peer(i)
+        remote(
+            whole.at[py, :, pc * SIDE_X + px, :, second],
+            near.at[:, chip, c],
+            send_near,
+            recv_near,
+            (px, py, z, pc),
+        ).start()
+
+    def hand_on(source, py, dy, t):
         @pl.loop(jnp.where(dy == 0, 1, 0), CORES * SIDE_X)
         def _(j):
             px = lax.rem(x + lax.rem(j, SIDE_X), SIDE_X)
             pc = lax.rem(c + j // SIDE_X, CORES)
             remote(
-                source.at[pc * SIDE_X + px],
-                own.at[:, links_of(block, size)],
-                send_p,
-                recv_p,
+                source(pc * SIDE_X + px),
+                own.at[chip, t, c, :, first],
+                send_last,
+                recv_last,
                 (px, py, z, pc),
             ).start()
 
         @pl.when(dy == 0)
         def _():
-            own[:, links_of(block, size)] = source[c * SIDE_X + x]
+            own[chip, t, c, :, first] = source(seat)[...]
 
     @pl.loop(0, SIDE_Y)
     def _(dy):
         py = lax.rem(y + dy, SIDE_Y)
-        hand_on(whole.at[py, z], py, dy, block_of(x, y, z, c))
-
-    @pl.loop(0, SIDE_Z - 1)
-    def _(k):
+        hand_on(lambda s: whole.at[py, z, s, :, first], py, dy, z)
+
+    @pl.loop(0, SIDE_Z)
+    def _(t):
+        near[t, chip, c] = whole[y, t, seat, :, second]
+
+    def take(k):
         t = lax.rem(z + SIDE_Z - along(k), SIDE_Z)
 
         @pl.loop(0, SIDE_Y)
         def _(dy):
             py = lax.rem(y + dy, SIDE_Y)
-            no_matter(stage.at[t, py], send_z, recv_z.at[t, py]).wait_recv()
-            hand_on(stage.at[t, py], py, dy, block_of(x, y, t, c))
-
-    no_matter(stage.at[pl.ds(0, SIDE_Z - 1)], send_z, recv_z.at[0, 0]).wait_send()
-    no_matter(own.at[:, pl.ds(0, (PLANE - 1) * SIDE_Z * size)], send_p, recv_p).wait()
+            no_matter(far.at[t * SIDE_Y + py], send_far, arrived.at[t, py]).wait_recv()
+            hand_on(lambda s: far.at[t * SIDE_Y + py, s], py, dy, t)
+
+    pl.loop(0, HALFWAY)(take)
+    chips = SIDE_X * SIDE_Y
+    others = far.at[pl.ds(0, PLANE - 1)]
+    no_matter(others, send_near, recv_near).wait()
+
+    @pl.loop(0, SIDE_Z - 1)
+    def _(k):
+        t = lax.rem(z + along(k), SIDE_Z)
+        remote(
+            near.at[t], own.at[:, z, :, :, second], send_own, recv_own, (x, y, t, c)
+        ).start()
+
+    @pl.loop(0, chips)
+    def _(i):
+        own[i, z, :, :, second] = near[z, i]
+
+    pl.loop(HALFWAY, SIDE_Z - 1)(take)
+    no_matter(far.at[pl.ds(0, (SIDE_Z - 1) * SIDE_Y)], send_far, recv_near).wait_send()
+    no_matter(near.at[pl.ds(0, SIDE_Z - 1)], send_own, recv_own).wait()
+    no_matter(others, send_last, recv_last).wait()
 
 
 VMEM = pl.BlockSpec(memory_space=pltpu.VMEM)
@@ -386,6 +439,7 @@
             pltpu.SemaphoreType.DMA((9,)),
             pltpu.SemaphoreType.DMA((9,)),
             pltpu.SemaphoreType.DMA((SIDE_Z,)),
+            pltpu.SemaphoreType.DMA((SIDE_X * SIDE_Y,)),
         ],
         compiler_params=pltpu.CompilerParams(
             collective_id=0, has_side_effects=True, vmem_limit_bytes=ROOM
@@ -395,18 +449,24 @@
 
 def scattered(high, low, state, own_rows):
     rows, size = state.shape
-    shape = (SIDE_Y, SIDE_Z, CORES * SIDE_X, own_rows, size)
+    cut = size // 2
+    chips, seats = SIDE_X * SIDE_Y, CORES * SIDE_X
     return pl.pallas_call(
         scatter_kernel,
         name="scatter",
-        out_shape=jax.ShapeDtypeStruct((own_rows, size * PLANE * SIDE_Z), state.dtype),
+        out_shape=jax.ShapeDtypeStruct((chips, SIDE_Z, CORES, own_rows, size), state.dtype),
         in_specs=[VMEM, VMEM, VMEM],
         out_specs=VMEM,
         scratch_shapes=[
-            pltpu.VMEM(shape, state.dtype),
-            pltpu.VMEM((SIDE_Z, SIDE_Y, *shape[2:]), state.dtype),
+            pltpu.VMEM((SIDE_Y, SIDE_Z, seats, own_rows, size), state.dtype),
+            pltpu.VMEM((PLANE, seats, own_rows, cut), state.dtype),
+            pltpu.VMEM((SIDE_Z, chips, CORES, own_rows, size - cut), state.dtype),
             pltpu.SemaphoreType.DMA,
             pltpu.SemaphoreType.DMA((SIDE_Z, SIDE_Y)),
+            pltpu.SemaphoreType.DMA,
+            pltpu.SemaphoreType.DMA,
+            pltpu.SemaphoreType.DMA,
+            pltpu.SemaphoreType.DMA,
             pltpu.SemaphoreType.DMA,
             pltpu.SemaphoreType.DMA,
         ],
@@ -672,20 +732,39 @@
     )(products.reshape(-1, TILE, TILE), sums)
 
 
-def put_out_kernel(own, out, done):
-    copy = pltpu.make_async_copy(own, out, done)
-    copy.start()
-    copy.wait()
+def put_out_kernel(own, out, laid, done):
+    size = own.shape[2]
+    share = own.shape[0] // PARTS
+
+    def part(k):
+        return links_of(k, share * size)
+
+    @pl.loop(0, PARTS)
+    def _(k):
+        for i in range(share):
+            laid[:, links_of(k * share + i, size)] = own[k * share + i]
+
+        pltpu.make_async_copy(laid.at[:, part(k)], out.at[:, part(k)], done.at[k]).start()
+
+    @pl.loop(0, PARTS)
+    def _(k):
+        pltpu.make_async_copy(laid.at[:, part(k)], out.at[:, part(k)], done.at[k]).wait()
+
+
+PARTS = 8
 
 
 def put_out(own):
+    rows, size = own.shape[-2:]
+    own = own.reshape(-1, rows, size)
+    shape = (rows, len(own) * size)
     return pl.pallas_call(
         put_out_kernel,
         name="put_out",
-        out_shape=jax.ShapeDtypeStruct(own.shape, own.dtype),
+        out_shape=jax.ShapeDtypeStruct(shape, own.dtype),
         in_specs=[VMEM],
         out_specs=pl.BlockSpec(memory_space=pltpu.HBM),
-        scratch_shapes=[pltpu.SemaphoreType.DMA],
+        scratch_shapes=[pltpu.VMEM(shape, own.dtype), pltpu.SemaphoreType.DMA((PARTS,))],
         compiler_params=pltpu.CompilerParams(vmem_limit_bytes=ROOM),
     )(own)
 

time: 181 us -> 175 us (0.967)
  Pallas kernels: 181 us -> 174 us
    pallas_call x1, Pallas kernels: 35.8 us -> 28.8 us  [scattered(): pl.pallas_call(scatter_kernel, name='scatter', out_shape=jax.ShapeDtypeSt...]
where the time goes in v5:
time: 175 us; the launch traced here: 174 us
  Pallas kernels  174 us (99%)
    pallas_call x1, Pallas kernels, mixed(): pl.pallas_call(mixing_kernel, name='mixing', out_shape=[jax.ShapeDtypeStr...  92.6 us
    pallas_call x1, Pallas kernels, gathered(): pl.pallas_call(gather_kernel, name='gather', out_shape=(jax.ShapeDtypeStr...  52 us
    pallas_call x1, Pallas kernels, scattered(): pl.pallas_call(scatter_kernel, name='scatter', out_shape=jax.ShapeDtypeSt...  28.8 us

profile of v5, /device:TPU:1, one launch (start us, length us, event | category | flops | bytes accessed | tf_op | source)
XLA Modules:
  0.0 174.5 jit_solution(3783355390912345215)
XLA Ops:
  0.0 52.0 %gather.1 = (bf16[4,8,16,1024]{3,2,1,0:T(8,128)(2,1)S(1)}, f32[2,640,128]{2,1,0:T(8,128)S(1)}, f32[2,512]{1,0:T(2,128)S(1)}) custom-call(bf16[2,262144]{1,0:T(2,128)(2,1)} %ensemble.1, s32[1,1,16]{2,1,0:T(1,128)} %offsets.1, f32[1,1,16]{2,1,0:T(1,128)} %observed.1, f32[1,1,16]{2,1,0:T(1,128)} %variances.1), custom_call_target="tpu_custom_call" | custom-call | tf_op jit(solution)/shard_map/gather/pallas_call | solution.py:414
  52.0 92.6 %mixing.1 = (bf16[512,512]{1,0:T(8,128)(2,1)S(1)}, bf16[512,512]{1,0:T(8,128)(2,1)S(1)}) custom-call(f32[10,128,128]{2,1,0:T(8,128)S(1)} %bitcast.5, f32[2,512]{1,0:T(2,128)S(1)} %get-tuple-element.11.sums), custom_call_target="tpu_custom_call" | custom-call | tf_op jit(solution)/shard_map/mixing/pallas_call | solution.py:718
  144.6 28.8 %scatter.1 = bf16[16,8,2,2,1024]{4,3,2,1,0:T(2,128)(2,1)S(1)} custom-call(bf16[512,512]{1,0:T(8,128)(2,1)S(1)} %get-tuple-element.12.high, bf16[512,512]{1,0:T(8,128)(2,1)S(1)} %get-tuple-element.13.low, bf16[512,1024]{1,0:T(8,128)(2,1)S(1)} %bitcast.4), custom_call_target="tpu_custom_call" | custom-call | tf_op jit(solution)/shard_map/scatter/pallas_call | solution.py:454
  173.4 1.1 put_out.1

commit v6 on v5

--- a/solution.py
+++ b/solution.py
@@ -100,13 +100,14 @@
 
 
 EARLY = 2
+HALVES = 2
 HALFWAY = 4
 
 
 def gather_kernel(
     ensemble, offsets, observed, variances, whole, total, sums,
-    own, notes, numbers, pieces, stage, all_notes, seen, picked, product, half, chunks, extras,
-    other, copied, send, recv, arrived, parted,
+    own, notes, numbers, pieces, stage, all_notes, seen, picked, half, chunks, extras,
+    twin, tables, anomalies, weighted, copied, send, recv, arrived, parted,
 ):
     x, y, z, c = here()
     size = own.shape[1] // (PLANE * SIDE_Z)
@@ -164,15 +165,18 @@
     no_matter(all_notes.at[pl.ds(0, SIDE_Z - 1)], send.at[0], recv.at[0]).wait()
     table = jnp.sum(all_notes[pl.ds(0, SIDE_Z)], axis=0)
     offset = table[0:1, :].astype(jnp.int32)
-    measured = table[1:2, :]
-    variance = table[2:3, :]
+    tables[c] = table
+    remote(tables.at[c], tables.at[c], send.at[9], recv.at[9], (x, y, z, 1 - c)).start()
     link = lax.broadcasted_iota(jnp.int32, (size, watches), 0)
     seen[...] = jnp.where(link == offset, 1.0, 0.0).astype(jnp.bfloat16)
     line = lax.broadcasted_iota(jnp.int32, (members // SIDE_Z, watches), 1) // count
 
-    def pass_on(k):
+    def pass_on(k, part):
         t = lax.rem(z + along(k), SIDE_Z)
-        remote(stage.at[t], whole.at[:, z], send.at[3], recv.at[3], (x, y, t, c)).start()
+        some = pl.ds(part * (SIDE_Y // 2), SIDE_Y // 2)
+        remote(
+            stage.at[t, some], whole.at[some, z], send.at[3], recv.at[3], (x, y, t, c)
+        ).start()
 
     def pick(k, found):
         t = lax.rem(z + along(k), SIDE_Z)
@@ -188,9 +192,13 @@
         rows = stage[t].reshape(members // SIDE_Z, size)
         values = jnp.dot(rows, seen[...], preferred_element_type=jnp.float32)
 
+        @pl.when(jnp.logical_and(k >= 1, k <= EARLY + HALVES))
+        def _():
+            pass_on(k - 1, 0)
+
         @pl.when(jnp.logical_and(k >= 1, k <= EARLY))
         def _():
-            pass_on(k - 1)
+            pass_on(k - 1, 1)
 
         return jnp.where(line == t, values, found)
 
@@ -202,9 +210,14 @@
     def _(i):
         remote(mine, picked.at[z], send.at[2], recv.at[2], line_peer(i)).start()
 
-    @pl.loop(EARLY, SIDE_Z - 1)
+    @pl.loop(EARLY, EARLY + HALVES)
     def _(k):
-        pass_on(k)
+        pass_on(k, 1)
+
+    @pl.loop(EARLY + HALVES, SIDE_Z - 1)
+    def _(k):
+        pass_on(k, 0)
+        pass_on(k, 1)
 
     picked[z] = mine[...]
     whole[:, z] = stage[z]
@@ -213,12 +226,23 @@
     ).wait_send()
     no_matter(picked.at[pl.ds(0, SIDE_Z - 1)], send.at[2], recv.at[2]).wait()
 
-    values = jnp.swapaxes(picked[pl.ds(0, SIDE_Z)], 0, 1).reshape(members, watches)
-    values = values.astype(jnp.float32)
-    center = jnp.sum(values, axis=0, keepdims=True) * (1.0 / members)
-    anomaly = values - center
-    innovation = measured - center
-    weight = 1.0 / ((members - 1.0) * variance)
+    partner = (x, y, z, 1 - c)
+    near = picked.at[pl.ds(0, SIDE_Z)]
+    remote(near, twin, send.at[4], recv.at[4], partner).start()
+
+    def terms(found, facts, core):
+        measured, variance = facts[1:2, :], facts[2:3, :]
+        values = jnp.swapaxes(found, 0, 1).reshape(members, watches).astype(jnp.float32)
+        center = jnp.sum(values, axis=0, keepdims=True) * (1.0 / members)
+        anomaly = values - center
+        innovation = measured - center
+        weight = 1.0 / ((members - 1.0) * variance)
+        at = links_of(core, watches)
+        anomalies[:, at] = anomaly
+        weighted[:, at] = anomaly * weight
+        return anomaly, innovation, weight, variance
+
+    anomaly, innovation, weight, variance = terms(picked[pl.ds(0, SIDE_Z)], table, c)
     spread = jnp.sum(anomaly * anomaly, axis=0, keepdims=True) * (1.0 / (members - 1.0)) + variance
     column = dot6_t(weight * innovation, anomaly)
     numer = jnp.sum(innovation * innovation, axis=1, keepdims=True)
@@ -227,18 +251,6 @@
     extra = extras.at[PLANE]
     extra[0:1, :] = column
     extra[1:2, :] = jnp.where(lane == 0, numer, jnp.where(lane == 1, denom, 0.0))
-    weighted = anomaly * weight
-    block = 0
-    for i in range(members // TILE):
-        row = dot6_t(weighted[i * TILE : (i + 1) * TILE], anomaly[: (i + 1) * TILE])
-        for j in range(i + 1):
-            core, at = divmod(block, product.shape[1] // TILE)
-            product[core, at * TILE : (at + 1) * TILE, :] = row[:, j * TILE : (j + 1) * TILE]
-            block += 1
-
-    rows = product.shape[1]
-    partner = (x, y, z, 1 - c)
-    remote(product.at[1 - c], other, send.at[4], recv.at[4], partner).start()
 
     @pl.loop(1, PLANE)
     def _(i):
@@ -247,8 +259,21 @@
         ).start()
 
     extras[y * (CORES * SIDE_X) + seat] = extra[...]
-    no_matter(other, send.at[4], recv.at[4]).wait()
-    half[...] = product[c] + other[...]
+    no_matter(tables.at[0], send.at[9], recv.at[9]).wait()
+    no_matter(twin, send.at[4], recv.at[4]).wait()
+    terms(twin[...], tables[1 - c], 1 - c)
+
+    tiles = members // TILE
+    blocks = [(i, j) for i in range(tiles) for j in range(i + 1)]
+    rows = half.shape[0]
+    count = rows // TILE
+    for k in range(count):
+        (i0, j0), (i1, j1) = blocks[k], blocks[count + k]
+        i, j = jnp.where(c == 0, i0, i1), jnp.where(c == 0, j0, j1)
+        half[k * TILE : (k + 1) * TILE, :] = dot6_t(
+            weighted[links_of(i, TILE), :], anomalies[links_of(j, TILE), :]
+        )
+
     chips = SIDE_X * SIDE_Y
     part = rows // chips
 
@@ -288,7 +313,7 @@
     no_matter(half.at[pl.ds(0, rows - part)], send.at[7], recv.at[7]).wait_send()
     no_matter(extras.at[pl.ds(0, PLANE - 1)], send.at[5], recv.at[5]).wait()
     sums[...] = jnp.sum(extras[pl.ds(0, PLANE)], axis=0)
-    no_matter(other, send.at[8], recv.at[8]).wait()
+    no_matter(half, send.at[8], recv.at[8]).wait()
     no_matter(stage.at[pl.ds(0, SIDE_Z - 1)], send.at[3], recv.at[3]).wait()
 
 
@@ -305,12 +330,13 @@
     greet(barrier)
     wide = 256
 
-    @pl.loop(0, size // wide)
-    def _(k):
+
+    def analyse(k):
         at = links_of(k, wide)
         values = dot1(high[...], state[:, at]) + dot1(low[...], state[:, at])
         whole[:, :, :, :, at] = values.astype(jnp.bfloat16).reshape(*whole.shape[:-1], wide)
 
+    pl.loop(0, size // wide)(analyse)
     met(barrier)
 
     @pl.loop(0, SIDE_Z - 1)
@@ -430,14 +456,16 @@
             pltpu.VMEM((SIDE_Z + 1, 8, watches), f32),
             pltpu.VMEM((size, watches), bf16),
             pltpu.VMEM((SIDE_Z + 1, SIDE_Y, seats * rows, watches), bf16),
-            pltpu.VMEM((CORES, packed, TILE), f32),
             pltpu.VMEM((packed, TILE), f32),
             pltpu.VMEM((SIDE_X * SIDE_Y, part, TILE), f32),
             pltpu.VMEM((PLANE + 1, 2, members), f32),
-            pltpu.VMEM((packed, TILE), f32),
+            pltpu.VMEM((SIDE_Z, SIDE_Y, seats * rows, watches), bf16),
+            pltpu.VMEM((CORES, 8, watches), f32),
+            pltpu.VMEM((members, CORES * watches), f32),
+            pltpu.VMEM((members, CORES * watches), f32),
             pltpu.SemaphoreType.DMA((4,)),
-            pltpu.SemaphoreType.DMA((9,)),
-            pltpu.SemaphoreType.DMA((9,)),
+            pltpu.SemaphoreType.DMA((10,)),
+            pltpu.SemaphoreType.DMA((10,)),
             pltpu.SemaphoreType.DMA((SIDE_Z,)),
             pltpu.SemaphoreType.DMA((SIDE_X * SIDE_Y,)),
         ],
@@ -536,7 +564,9 @@
     parts[pl.ds(rows, rows), :] = (values - high.astype(jnp.float32)).astype(jnp.bfloat16)
     top = pl.ds(0, n)
     r[...] = passes(parts[top, :], parts[top, :])
-    bound = jnp.sqrt(jnp.max(jnp.sum(jnp.abs(r[...]), axis=0, keepdims=True)) * 1.02)
+    square = r[...].astype(jnp.bfloat16)
+    fourth = jnp.max(jnp.sum(jnp.abs(passes(square, square)), axis=0, keepdims=True))
+    bound = jnp.sqrt(jnp.sqrt(fourth * 1.05))
     a = 2.0 / (1.0 + bound)
 
     def first(rows, total):

time: 175 us -> 174 us (level)
  no operation moved by 1% of the time
where the time goes in v6:
time: 174 us
  Pallas kernels  174 us (100%)
    pallas_call x1, Pallas kernels, mixed(): pl.pallas_call(mixing_kernel, name='mixing', out_shape=[jax.ShapeDtypeStr...  92.6 us
    pallas_call x1, Pallas kernels, gathered(): pl.pallas_call(gather_kernel, name='gather', out_shape=(jax.ShapeDtypeStr...  51.1 us
    pallas_call x1, Pallas kernels, scattered(): pl.pallas_call(scatter_kernel, name='scatter', out_shape=jax.ShapeDtypeSt...  29.2 us

profile of v6, /device:TPU:1, one launch (start us, length us, event | category | flops | bytes accessed | tf_op | source)
XLA Modules:
  0.0 174.1 jit_solution(7076293347400590452)
XLA Ops:
  0.0 51.1 %gather.1 = (bf16[4,8,16,1024]{3,2,1,0:T(8,128)(2,1)S(1)}, f32[2,640,128]{2,1,0:T(8,128)S(1)}, f32[2,512]{1,0:T(2,128)S(1)}) custom-call(bf16[2,262144]{1,0:T(2,128)(2,1)} %ensemble.1, s32[1,1,16]{2,1,0:T(1,128)} %offsets.1, f32[1,1,16]{2,1,0:T(1,128)} %observed.1, f32[1,1,16]{2,1,0:T(1,128)} %variances.1), custom_call_target="tpu_custom_call" | custom-call | tf_op jit(solution)/shard_map/gather/pallas_call | solution.py:440
  51.1 92.6 %mixing.1 = (bf16[512,512]{1,0:T(8,128)(2,1)S(1)}, bf16[512,512]{1,0:T(8,128)(2,1)S(1)}) custom-call(f32[10,128,128]{2,1,0:T(8,128)S(1)} %bitcast.5, f32[2,512]{1,0:T(2,128)S(1)} %get-tuple-element.11.sums), custom_call_target="tpu_custom_call" | custom-call | tf_op jit(solution)/shard_map/mixing/pallas_call | solution.py:748
  143.7 29.2 %scatter.1 = bf16[16,8,2,2,1024]{4,3,2,1,0:T(2,128)(2,1)S(1)} custom-call(bf16[512,512]{1,0:T(8,128)(2,1)S(1)} %get-tuple-element.12.high, bf16[512,512]{1,0:T(8,128)(2,1)S(1)} %get-tuple-element.13.low, bf16[512,1024]{1,0:T(8,128)(2,1)S(1)} %bitcast.4), custom_call_target="tpu_custom_call" | custom-call | tf_op jit(solution)/shard_map/scatter/pallas_call | solution.py:482
  173.0 1.1 put_out.1

commit v7 on v6

--- a/solution.py
+++ b/solution.py
@@ -328,7 +328,7 @@
     first, second = pl.ds(0, cut), pl.ds(cut, size - cut)
     barrier = pltpu.get_barrier_semaphore()
     greet(barrier)
-    wide = 256
+    wide = 512
 
 
     def analyse(k):

time: 174 us -> 174 us (level)
  no operation moved by 1% of the time
where the time goes in v7:
time: 174 us
  Pallas kernels  174 us (100%)
    pallas_call x1, Pallas kernels, mixed(): pl.pallas_call(mixing_kernel, name='mixing', out_shape=[jax.ShapeDtypeStr...  92.6 us
    pallas_call x1, Pallas kernels, gathered(): pl.pallas_call(gather_kernel, name='gather', out_shape=(jax.ShapeDtypeStr...  51.1 us
    pallas_call x1, Pallas kernels, scattered(): pl.pallas_call(scatter_kernel, name='scatter', out_shape=jax.ShapeDtypeSt...  29.2 us

profile of v7, /device:TPU:1, one launch (start us, length us, event | category | flops | bytes accessed | tf_op | source)
XLA Modules:
  0.0 174.1 jit_solution(14091523352054632632)
XLA Ops:
  0.0 51.1 %gather.1 = (bf16[4,8,16,1024]{3,2,1,0:T(8,128)(2,1)S(1)}, f32[2,640,128]{2,1,0:T(8,128)S(1)}, f32[2,512]{1,0:T(2,128)S(1)}) custom-call(bf16[2,262144]{1,0:T(2,128)(2,1)} %ensemble.1, s32[1,1,16]{2,1,0:T(1,128)} %offsets.1, f32[1,1,16]{2,1,0:T(1,128)} %observed.1, f32[1,1,16]{2,1,0:T(1,128)} %variances.1), custom_call_target="tpu_custom_call" | custom-call | tf_op jit(solution)/shard_map/gather/pallas_call | solution.py:440
  51.1 92.6 %mixing.1 = (bf16[512,512]{1,0:T(8,128)(2,1)S(1)}, bf16[512,512]{1,0:T(8,128)(2,1)S(1)}) custom-call(f32[10,128,128]{2,1,0:T(8,128)S(1)} %bitcast.5, f32[2,512]{1,0:T(2,128)S(1)} %get-tuple-element.11.sums), custom_call_target="tpu_custom_call" | custom-call | tf_op jit(solution)/shard_map/mixing/pallas_call | solution.py:748
  143.7 29.2 %scatter.1 = bf16[16,8,2,2,1024]{4,3,2,1,0:T(2,128)(2,1)S(1)} custom-call(bf16[512,512]{1,0:T(8,128)(2,1)S(1)} %get-tuple-element.12.high, bf16[512,512]{1,0:T(8,128)(2,1)S(1)} %get-tuple-element.13.low, bf16[512,1024]{1,0:T(8,128)(2,1)S(1)} %bitcast.4), custom_call_target="tpu_custom_call" | custom-call | tf_op jit(solution)/shard_map/scatter/pallas_call | solution.py:482
  173.0 1.1 put_out.1
